TPU v7x, 256 devices: a whole 4x4x8 slice. The times are simulated.
256 devices in a mesh: edge: 64 (over y, z, x_lo), chan: 4 (over x_hi, core).
Axes of the slice: x: 4 (x_hi: 2, x_lo: 2; x = x_hi * 2 + x_lo), y: 4, z: 8, core: 2. Of those that a mesh axis runs over, the one named last changes fastest.
Arguments:
- node_states: bfloat16 [1024, 49, 256], P('edge', None, 'chan'), may hold values from -6 to 6
- edge_vectors: float32 [3, 32768], P(None, ('edge', 'chan')), may hold values from -5.6 to 5.6, as said below
- source_part: int32 [32768, 1], P('edge'), may hold values from 0 to 63; in each aligned block of 512 rows (0 to 511, 512 to 1023, ...) at most 16 rows name the same one
- source_slot: int32 [32768], P('edge'), may hold values from 0 to 15
- target_slot: int32 [32768], P('edge'), may hold values from 0 to 15
- live_edges: int32 [64], P('edge'), may hold values from 1 to 512, 24576 in all
- weight_zero: bfloat16 [7, 256, 7, 256], P(None, 'chan'), may hold values from -0.125 to 0.125
- weight_one: bfloat16 [2, 6, 256, 6, 256], P(None, None, 'chan'), may hold values from -0.109375 to 0.109375
- weight_two: bfloat16 [2, 5, 256, 5, 256], P(None, None, 'chan'), may hold values from -0.125 to 0.125
Outputs:
- aggregated: bfloat16 [1024, 49, 256], P('edge', None, 'chan')
Inputs may be any that keep to these rules, and one draw needn't show every extreme that they name: `source_part`: in each aligned block of 512 rows (the edges of one partition's slab) no partition number appears more than 16 times, and some number appears exactly 16 times. Edges are grouped by destination partition: the destination of an edge in slab p is node p * 16 + target_slot. `live_edges`: live slots stand at the front of each slab; the fullest slab is full. `edge_vectors`: every column has length between 0.8 and 5.6.
All inputs are finite; a program needn't handle non-finite values. No bound on the sum of `live_edges` on one device may be relied on, other than what follows from the above.
Results may differ from a plain program's by a relative error of at most 0.015.
Values may be sent and summed in bfloat16 or wider, within the bound.
A program may use at most 128 MiB of HBM per device.

v0:
```python
import math

import jax
import jax.numpy as jnp
import numpy as np
from jax import lax
from jax.sharding import PartitionSpec as P

LMAX = 6
MMAX = 2


cutoff_radius = 6.0
highest = lax.Precision.HIGHEST


def harmonics(coord_x, coord_y, coord_z, degree_top, order_top):
    results = {}
    real_part = [coord_x * 0.0 + 1.0]
    imag_part = [coord_x * 0.0]
    for azimuthal in range(1, order_top + 1):
        new_real = coord_x * real_part[-1] - coord_y * imag_part[-1]
        new_imag = coord_x * imag_part[-1] + coord_y * real_part[-1]
        real_part.append(new_real)
        imag_part.append(new_imag)
    for azimuthal in range(order_top + 1):
        start_value = (-1.0) ** azimuthal * math.prod(range(2 * azimuthal - 1, 0, -2))
        legendre = {azimuthal: coord_z * 0.0 + start_value}
        if azimuthal + 1 <= degree_top:
            legendre[azimuthal + 1] = coord_z * ((2 * azimuthal + 1) * start_value)
        for degree in range(azimuthal + 2, degree_top + 1):
            legendre[degree] = (
                (2 * degree - 1) * coord_z * legendre[degree - 1]
                - (degree + azimuthal - 1) * legendre[degree - 2]
            ) / (degree - azimuthal)
        for degree in range(azimuthal, degree_top + 1):
            factor = math.sqrt(
                (2 * degree + 1)
                / (4.0 * math.pi)
                * math.factorial(degree - azimuthal)
                / math.factorial(degree + azimuthal)
            )
            if azimuthal == 0:
                results[degree, 0] = factor * legendre[degree]
            else:
                results[degree, azimuthal] = (
                    math.sqrt(2.0) * factor * legendre[degree] * real_part[azimuthal]
                )
                results[degree, -azimuthal] = (
                    math.sqrt(2.0) * factor * legendre[degree] * imag_part[azimuthal]
                )
    return results


def kept_rows():
    row_list = [(degree, 0) for degree in range(LMAX + 1)]
    for azimuthal in range(1, MMAX + 1):
        row_list += [(degree, azimuthal) for degree in range(azimuthal, LMAX + 1)]
        row_list += [(degree, -azimuthal) for degree in range(azimuthal, LMAX + 1)]
    return row_list


def row_offsets():
    listing = []
    offset = 0
    for degree, azimuthal in kept_rows():
        listing.append((degree, offset))
        offset += 2 * degree + 1
    return listing


def invert_small(matrix):
    order_size = matrix.shape[0]
    work = np.concatenate([matrix, np.eye(order_size)], axis=1)
    for column in range(order_size):
        work[column] = work[column] / work[column, column]
        for row_index in range(order_size):
            if row_index != column:
                work[row_index] = work[row_index] - work[row_index, column] * work[column]
    return work[:, order_size:]


def sample_tables():
    sample_count = 2 * (LMAX + 1) ** 2
    positions = np.arange(sample_count) + 0.5
    height = 1.0 - 2.0 * positions / sample_count
    radius = np.sqrt(1.0 - height * height)
    azimuth = math.pi * (3.0 - math.sqrt(5.0)) * positions
    points = np.stack([radius * np.cos(azimuth), radius * np.sin(azimuth), height])
    values = harmonics(points[0], points[1], points[2], LMAX, LMAX)
    inverses = []
    for degree in range(LMAX + 1):
        sampled = np.stack([values[degree, azimuthal] for azimuthal in range(-degree, degree + 1)])
        inverses.append(sampled.T @ invert_small(sampled @ sampled.T))
    return (points, inverses)


def wigner_rows(vectors):
    length = jnp.sqrt(jnp.sum(vectors * vectors, axis=0))
    direction = vectors / length
    pick_first = jnp.where(jnp.abs(direction[0]) < 0.6, 1.0, 0.0).astype(jnp.float32)
    helper = jnp.stack([pick_first, 1.0 - pick_first, jnp.zeros_like(pick_first)])
    first_axis = jnp.cross(direction, helper, axis=0)
    first_axis = first_axis / jnp.sqrt(jnp.sum(first_axis * first_axis, axis=0))
    second_axis = jnp.cross(direction, first_axis, axis=0)
    frames = jnp.stack([first_axis, second_axis, direction])
    points, inverses = sample_tables()
    sample = jnp.asarray(points, jnp.float32)
    turned = jnp.einsum("rce,ck->rek", frames, sample, precision=highest)
    values = harmonics(turned[0], turned[1], turned[2], LMAX, MMAX)
    pieces = []
    for degree, azimuthal in kept_rows():
        table = jnp.asarray(inverses[degree], jnp.float32)
        pieces.append(jnp.dot(values[degree, azimuthal], table, precision=highest))
    compact = jnp.concatenate(pieces, axis=1)
    envelope = 0.5 * (jnp.cos(math.pi * length / cutoff_radius) + 1.0)
    return (compact, envelope)


def rotate_forward(compact_t, sources):
    rows_out = []
    for degree, offset in row_offsets():
        total = compact_t[offset].astype(jnp.float32)[None, :] * sources[degree * degree].astype(
            jnp.float32
        )
        for inner in range(1, 2 * degree + 1):
            total = total + compact_t[offset + inner].astype(jnp.float32)[None, :] * sources[
                degree * degree + inner
            ].astype(jnp.float32)
        rows_out.append(total)
    return jnp.stack(rows_out, axis=0).astype(jnp.bfloat16)


def rotate_back(compact_t, scaled):
    listing = row_offsets()
    coefs_out = []
    for degree in range(LMAX + 1):
        for inner in range(2 * degree + 1):
            total = None
            for row_index, (row_degree, offset) in enumerate(listing):
                if row_degree == degree:
                    term = compact_t[offset + inner].astype(jnp.float32)[None, :] * scaled[
                        :, row_index
                    ].astype(jnp.float32)
                    total = term if total is None else total + term
            coefs_out.append(total)
    return jnp.stack(coefs_out, axis=0).astype(jnp.bfloat16)


def convolve(turned, weight_zero, weight_one, weight_two, contract):
    end_zero = LMAX + 1
    end_one_plus = end_zero + LMAX
    end_one_minus = end_one_plus + LMAX
    end_two_plus = end_one_minus + LMAX - 1
    zero_part = turned[:end_zero]
    one_plus = turned[end_zero:end_one_plus]
    one_minus = turned[end_one_plus:end_one_minus]
    two_plus = turned[end_one_minus:end_two_plus]
    two_minus = turned[end_two_plus:]
    pattern = "lce,lcjd->dje"
    out_zero = contract(pattern, zero_part, weight_zero)
    out_one_plus = contract(pattern, one_plus, weight_one[0]) - contract(
        pattern, one_minus, weight_one[1]
    )
    out_one_minus = contract(pattern, one_minus, weight_one[0]) + contract(
        pattern, one_plus, weight_one[1]
    )
    out_two_plus = contract(pattern, two_plus, weight_two[0]) - contract(
        pattern, two_minus, weight_two[1]
    )
    out_two_minus = contract(pattern, two_minus, weight_two[0]) + contract(
        pattern, two_plus, weight_two[1]
    )
    return jnp.concatenate(
        [out_zero, out_one_plus, out_one_minus, out_two_plus, out_two_minus], axis=1
    )


def mixed_contract(pattern, first_operand, second_operand):
    return jnp.einsum(pattern, first_operand, second_operand, preferred_element_type=jnp.float32)


def one_hot(indices, width):
    return (indices[:, None] == jnp.arange(width, dtype=jnp.int32)[None, :]).astype(jnp.bfloat16)


def pick_columns(table, selector):
    picked = lax.dot_general(
        table, selector, (((0,), (1,)), ((), ())), preferred_element_type=jnp.float32
    )
    return picked.astype(jnp.bfloat16)


def pick_rows(selector, table):
    return jnp.dot(selector, table, preferred_element_type=jnp.float32).astype(jnp.bfloat16)


def shards(
    node_states,
    edge_vectors,
    source_part,
    source_slot,
    target_slot,
    live_edges,
    weight_zero,
    weight_one,
    weight_two,
):
    slab_size = source_slot.shape[0]
    local_nodes = node_states.shape[0]
    local_channels = node_states.shape[2]
    coef_count = node_states.shape[1]
    group_count = lax.axis_size("edge")
    capacity = max(2, 2 * slab_size // group_count)
    slot_total = group_count * capacity
    quarter, quarter_fade = wigner_rows(edge_vectors)
    compact, envelope = (
        lax.all_gather(quarter.astype(jnp.bfloat16), "chan", axis=0, tiled=True),
        lax.all_gather(quarter_fade.astype(jnp.bfloat16), "chan", axis=0, tiled=True),
    )
    compact_t = compact.T
    node_flat = node_states.reshape(local_nodes, coef_count * local_channels)
    owner_part = source_part[:, 0]
    owners = jnp.arange(group_count, dtype=jnp.int32)
    member = (owner_part[:, None] == owners[None, :]).astype(jnp.int32)
    earlier = jnp.cumsum(member, axis=0) - member
    position = jnp.sum(earlier * member, axis=1)
    slot_flat = owner_part * capacity + position
    requests = (
        jnp.zeros((slot_total,), jnp.int32)
        .at[slot_flat]
        .set(source_slot)
        .reshape(group_count, capacity)
    )
    slot_select = one_hot(slot_flat, slot_total)
    wanted = lax.all_to_all(requests, "edge", split_axis=0, concat_axis=0, tiled=True)
    picked = pick_rows(one_hot(wanted.reshape(-1), local_nodes), node_flat)
    returned = lax.all_to_all(
        picked.reshape(group_count, capacity, coef_count * local_channels),
        "edge",
        split_axis=0,
        concat_axis=0,
        tiled=True,
    )
    sources = pick_columns(
        returned.reshape(slot_total, coef_count * local_channels), slot_select
    ).reshape(coef_count, local_channels, slab_size)
    turned = rotate_forward(compact_t, sources)
    channel_mix = lax.psum_scatter(
        convolve(turned, weight_zero, weight_one, weight_two, mixed_contract).astype(jnp.bfloat16),
        "chan",
        scatter_dimension=0,
        tiled=True,
    ).astype(jnp.float32)
    alive_mask = (jnp.arange(slab_size, dtype=jnp.int32) < live_edges[0]).astype(jnp.float32)
    scaling = envelope.astype(jnp.float32) * alive_mask
    scaled = (channel_mix * scaling).astype(jnp.bfloat16)
    message = rotate_back(compact_t, scaled).reshape(coef_count * local_channels, slab_size)
    selector = (jnp.arange(local_nodes, dtype=jnp.int32)[:, None] == target_slot[None, :]).astype(
        jnp.bfloat16
    )
    summed = lax.dot_general(
        selector, message, (((1,), (1,)), ((), ())), preferred_element_type=jnp.float32
    )
    return summed.astype(jnp.bfloat16).reshape(local_nodes, coef_count, local_channels)


def solution(mesh):
    in_specs = (
        P("edge", None, "chan"),
        P(None, ("edge", "chan")),
        P("edge", None),
        P("edge"),
        P("edge"),
        P("edge"),
        P(None, "chan", None, None),
        P(None, None, "chan", None, None),
        P(None, None, "chan", None, None),
    )
    out_specs = P("edge", None, "chan")
    return jax.shard_map(shards, mesh=mesh, in_specs=in_specs, out_specs=out_specs, check_vma=False)
```

profile of v0, /device:TPU:1, one launch (start us, length us, event | category | flops | bytes accessed | tf_op | source)
XLA Modules:
  0.0 345.9 jit_solution(5656310908398579439)
XLA Ops:
  6.5 0.8 fusion.497
  7.4 1.2 reduce-window.6
  9.6 1.3 compare_select_fusion
  10.9 2.6 scatter_custom_fusion
  14.2 13.6 %all-to-all-start = ((s32[64,1,16]{2,1,0:T(1,128)}), s32[64,1,16]{2,1,0:T(1,128)S(1)}, u32[]{:S(2)}, u32[]{:S(2)}) async-start(s32[64,1,16]{2,1,0:T(1,128)} %bitcast.27), calls=%async_computation | async-start | bytes 65536 | tf_op jit(solution)/shard_map/all_to_all | solution.py:236
  28.5 1.0 copy.58
  29.7 7.3 %all-to-all-done = s32[64,1,16]{2,1,0:T(1,128)S(1)} async-done(((s32[64,1,16]{2,1,0:T(1,128)}), s32[64,1,16]{2,1,0:T(1,128)S(1)}, u32[]{:S(2)}, u32[]{:S(2)}) %all-to-all-start) | async-done | bytes 4128 | tf_op jit(solution)/shard_map/all_to_all | solution.py:236
  38.3 4.7 %convolution_convert_fusion = bf16[1024,3136]{0,1:T(8,128)(2,1)} fusion(bf16[16,3136]{1,0:T(8,128)(2,1)S(1)} %reshape.10748, s32[1024]{0:T(1024)S(1)} %eq.79), kind=kOutput, calls=%fused_computation.1 | convolution fusion | flops 105988096 | bytes 6526976 | tf_op jit(solution)/shard_map/dot_general | solution.py:195
  42.9 9.3 %copy.59 = bf16[1024,3136]{1,0:T(8,128)(2,1)} copy(bf16[1024,3136]{0,1:T(8,128)(2,1)} %convolution_convert_fusion) | data formatting | bytes 12845056 | tf_op jit(solution)/shard_map/convert_element_type | solution.py:195
  52.3 5.8 %all-to-all-start.1 = ((bf16[64,16,3136]{2,1,0:T(8,128)(2,1)}), bf16[64,16,3136]{2,1,0:T(8,128)(2,1)}, u32[]{:S(2)}, u32[]{:S(2)}) async-start(bf16[64,16,3136]{2,1,0:T(8,128)(2,1)} %bitcast.1286), calls=%async_computation.1 | async-start | bytes 13107200 | tf_op jit(solution)/shard_map/all_to_all | solution.py:238
  66.5 2.1 concatenate.16
  68.6 9.9 %all_gather.6 = bf16[512,235]{0,1:T(8,128)(2,1)S(1)} all-gather(bf16[128,235]{0,1:T(8,128)(2,1)S(1)} %concatenate.16), channel_id=1, replica_groups=mesh['edge'=64,'chan'=4] {'chan'}, dimensions={0}, use_global_device_ids=true | all-gather | bytes 300800 | tf_op jit(solution)/shard_map/all_gather | solution.py:218
  86.3 1.3 fusion.803
  87.6 1.2 fusion.802
  88.8 113.9 %all-to-all-done.1 = bf16[64,16,3136]{2,1,0:T(8,128)(2,1)} async-done(((bf16[64,16,3136]{2,1,0:T(8,128)(2,1)}), bf16[64,16,3136]{2,1,0:T(8,128)(2,1)}, u32[]{:S(2)}, u32[]{:S(2)}) %all-to-all-start.1) | async-done | bytes 6422560 | tf_op jit(solution)/shard_map/all_to_all | solution.py:238
  203.0 7.0 %convolution_convert_fusion.1 = bf16[3136,512]{1,0:T(8,128)(2,1)S(1)} fusion(bf16[1024,3136]{1,0:T(8,128)(2,1)} %bitcast.29, s32[512]{0:T(512)} %bitcast.1775), kind=kOutput, calls=%fused_computation.2 | convolution fusion | flops 3290464256 | bytes 9635840 | tf_op jit(solution)/shard_map/dot_general | solution.py:188
  210.3 0.9 constant_dynamic-update-slice_fusion.17
  213.7 1.0 fusion.12
  215.9 1.0 fusion.11
  217.5 0.8 constant_dynamic-update-slice_fusion.21
  219.0 0.9 fusion.14
  220.8 0.9 fusion.13
  222.6 2.5 bitcast_dynamic-update-slice_fusion
  225.0 2.2 bitcast_dynamic-update-slice_fusion.2
  227.3 2.2 bitcast_dynamic-update-slice_fusion.1
  229.4 2.0 fusion.5
  231.4 1.9 fusion.7
  233.4 14.5 %copy.65 = bf16[256,29,512]{2,1,0:T(8,128)(2,1)} copy(bf16[256,29,512]{0,2,1:T(8,128)(2,1)} %fusion.7) | data formatting | bytes 15204352 | tf_op jit(solution)/shard_map/concatenate | solution.py:174
  248.5 9.3 %all-gather = bf16[4,1,128]{2,1,0:T(2,128)(2,1)S(1)} all-gather(bf16[1,1,128]{2,1,0:T(2,128)(2,1)S(1)} %copy-done.205), channel_id=1, replica_groups=mesh['edge'=64,'chan'=4] {'chan'}, dimensions={0}, use_global_device_ids=true | all-gather | bytes 1280 | tf_op jit(solution)/shard_map/all_gather | solution.py:219
  258.6 71.5 %reduce-scatter.2.cloned.1.call-done = bf16[64,29,512]{2,1,0:T(8,128)(2,1)} async-done(((bf16[256,29,512]{2,1,0:T(8,128)(2,1)}), bf16[64,29,512]{2,1,0:T(8,128)(2,1)}) %reduce-scatter.2.cloned.1.call-update) | async-done | bytes 1900560 | tf_op jit(solution)/shard_map/reduce_scatter | solution.py:249
  330.1 2.7 multiply_convert_fusion
  337.2 0.9 convolution_convert_fusion.2
  (566 shorter events, 30.0 us)
Async XLA Ops:
  6.5 216.0 %copy-start = (bf16[7,64,7,256]{3,1,2,0:T(8,128)(2,1)S(1)}, bf16[7,64,7,256]{3,1,2,0:T(8,128)(2,1)}, u32[]{:S(2)}) copy-start(bf16[7,64,7,256]{3,1,2,0:T(8,128)(2,1)} %param.47) | copy-start | bytes 4816900
  14.2 22.7 %all-to-all-start = ((s32[64,1,16]{2,1,0:T(1,128)}), s32[64,1,16]{2,1,0:T(1,128)S(1)}, u32[]{:S(2)}, u32[]{:S(2)}) async-start(s32[64,1,16]{2,1,0:T(1,128)} %bitcast.27), calls=%async_computation | async-start | bytes 65536 | tf_op jit(solution)/shard_map/all_to_all | solution.py:236
  52.3 150.4 %all-to-all-start.1 = ((bf16[64,16,3136]{2,1,0:T(8,128)(2,1)}), bf16[64,16,3136]{2,1,0:T(8,128)(2,1)}, u32[]{:S(2)}, u32[]{:S(2)}) async-start(bf16[64,16,3136]{2,1,0:T(8,128)(2,1)} %bitcast.1286), calls=%async_computation.1 | async-start | bytes 13107200 | tf_op jit(solution)/shard_map/all_to_all | solution.py:238
  58.1 272.0 %reduce-scatter.2.cloned.1.call-start = ((), (), s32[]{:S(2)}) async-start(), calls=%async_computation.3 | async-start | bytes 10485760 | tf_op jit(solution)/shard_map/reduce_scatter | solution.py:249
  62.2 24.0 %copy-start.3 = (bf16[2,5,64,5,256]{4,2,3,1,0:T(8,128)(2,1)S(1)}, bf16[2,5,64,5,256]{4,2,3,1,0:T(8,128)(2,1)}, u32[]{:S(2)}) copy-start(bf16[2,5,64,5,256]{4,2,3,1,0:T(8,128)(2,1)} %param.49) | copy-start | bytes 4915204
  68.5 19.0 %copy-start.2 = (bf16[2,6,64,6,256]{4,2,3,1,0:T(8,128)(2,1)S(1)}, bf16[2,6,64,6,256]{4,2,3,1,0:T(8,128)(2,1)}, u32[]{:S(2)}) copy-start(bf16[2,6,64,6,256]{4,2,3,1,0:T(8,128)(2,1)} %param.48) | copy-start | bytes 7077892
  202.9 10.1 %copy-start.12 = (f32[1,512]{1,0:T(1,128)S(1)}, f32[1,512]{1,0:T(1,128)}, u32[]{:S(2)}) copy-start(f32[1,512]{1,0:T(1,128)} %get-tuple-element.176) | copy-start | bytes 6148
  202.9 10.1 %copy-start.18 = (f32[1,512]{1,0:T(1,128)S(1)}, f32[1,512]{1,0:T(1,128)}, u32[]{:S(2)}) copy-start(f32[1,512]{1,0:T(1,128)} %get-tuple-element.177) | copy-start | bytes 6148
  202.9 10.1 %copy-start.25 = (f32[1,512]{1,0:T(1,128)S(1)}, f32[1,512]{1,0:T(1,128)}, u32[]{:S(2)}) copy-start(f32[1,512]{1,0:T(1,128)} %get-tuple-element.178) | copy-start | bytes 6148
  202.9 10.1 %copy-start.31 = (f32[1,512]{1,0:T(1,128)S(1)}, f32[1,512]{1,0:T(1,128)}, u32[]{:S(2)}) copy-start(f32[1,512]{1,0:T(1,128)} %get-tuple-element.179) | copy-start | bytes 6148
  202.9 10.1 %copy-start.37 = (f32[1,512]{1,0:T(1,128)S(1)}, f32[1,512]{1,0:T(1,128)}, u32[]{:S(2)}) copy-start(f32[1,512]{1,0:T(1,128)} %get-tuple-element.180) | copy-start | bytes 6148
  202.9 10.1 %copy-start.43 = (f32[1,512]{1,0:T(1,128)S(1)}, f32[1,512]{1,0:T(1,128)}, u32[]{:S(2)}) copy-start(f32[1,512]{1,0:T(1,128)} %get-tuple-element.181) | copy-start | bytes 6148
  203.0 10.1 %copy-start.49 = (f32[1,512]{1,0:T(1,128)S(1)}, f32[1,512]{1,0:T(1,128)}, u32[]{:S(2)}) copy-start(f32[1,512]{1,0:T(1,128)} %get-tuple-element.182) | copy-start | bytes 6148
  203.0 10.1 %copy-start.56 = (f32[1,512]{1,0:T(1,128)S(1)}, f32[1,512]{1,0:T(1,128)}, u32[]{:S(2)}) copy-start(f32[1,512]{1,0:T(1,128)} %get-tuple-element.183) | copy-start | bytes 6148
  247.9 85.1 %copy-start.164 = (f32[1,512]{1,0:T(1,128)S(1)}, f32[1,512]{1,0:T(1,128)}, u32[]{:S(2)}) copy-start(f32[1,512]{1,0:T(1,128)} %get-tuple-element.162) | copy-start | bytes 6148
  247.9 85.1 %copy-start.201 = (f32[1,512]{1,0:T(1,128)S(1)}, f32[1,512]{1,0:T(1,128)}, u32[]{:S(2)}) copy-start(f32[1,512]{1,0:T(1,128)} %get-tuple-element.208) | copy-start | bytes 6148
  247.9 85.2 %copy-start.158 = (f32[1,512]{1,0:T(1,128)S(1)}, f32[1,512]{1,0:T(1,128)}, u32[]{:S(2)}) copy-start(f32[1,512]{1,0:T(1,128)} %get-tuple-element.161) | copy-start | bytes 6148
  247.9 85.2 %copy-start.199 = (f32[1,512]{1,0:T(1,128)S(1)}, f32[1,512]{1,0:T(1,128)}, u32[]{:S(2)}) copy-start(f32[1,512]{1,0:T(1,128)} %get-tuple-element.210) | copy-start | bytes 6148
  247.9 85.2 %copy-start.152 = (f32[1,512]{1,0:T(1,128)S(1)}, f32[1,512]{1,0:T(1,128)}, u32[]{:S(2)}) copy-start(f32[1,512]{1,0:T(1,128)} %get-tuple-element.160) | copy-start | bytes 6148
  247.9 85.2 %copy-start.198 = (f32[1,512]{1,0:T(1,128)S(1)}, f32[1,512]{1,0:T(1,128)}, u32[]{:S(2)}) copy-start(f32[1,512]{1,0:T(1,128)} %get-tuple-element.209) | copy-start | bytes 6148
  247.9 85.3 %copy-start.144 = (f32[1,512]{1,0:T(1,128)S(1)}, f32[1,512]{1,0:T(1,128)}, u32[]{:S(2)}) copy-start(f32[1,512]{1,0:T(1,128)} %get-tuple-element.159) | copy-start | bytes 6148
  248.0 85.3 %copy-start.202 = (f32[1,512]{1,0:T(1,128)S(1)}, f32[1,512]{1,0:T(1,128)}, u32[]{:S(2)}) copy-start(f32[1,512]{1,0:T(1,128)} %get-tuple-element.207) | copy-start | bytes 6148
  248.0 85.4 %copy-start.134 = (f32[1,512]{1,0:T(1,128)S(1)}, f32[1,512]{1,0:T(1,128)}, u32[]{:S(2)}) copy-start(f32[1,512]{1,0:T(1,128)} %get-tuple-element.158) | copy-start | bytes 6148
  248.0 85.4 %copy-start.200 = (f32[1,512]{1,0:T(1,128)S(1)}, f32[1,512]{1,0:T(1,128)}, u32[]{:S(2)}) copy-start(f32[1,512]{1,0:T(1,128)} %get-tuple-element.206) | copy-start | bytes 6148
  248.0 85.5 %copy-start.126 = (f32[1,512]{1,0:T(1,128)S(1)}, f32[1,512]{1,0:T(1,128)}, u32[]{:S(2)}) copy-start(f32[1,512]{1,0:T(1,128)} %get-tuple-element.157) | copy-start | bytes 6148
  248.0 85.5 %copy-start.197 = (f32[1,512]{1,0:T(1,128)S(1)}, f32[1,512]{1,0:T(1,128)}, u32[]{:S(2)}) copy-start(f32[1,512]{1,0:T(1,128)} %get-tuple-element.205) | copy-start | bytes 6148
  248.0 85.6 %copy-start.196 = (f32[1,512]{1,0:T(1,128)S(1)}, f32[1,512]{1,0:T(1,128)}, u32[]{:S(2)}) copy-start(f32[1,512]{1,0:T(1,128)} %get-tuple-element.204) | copy-start | bytes 6148
  258.5 75.2 %copy-start.193 = (f32[1,512]{1,0:T(1,128)S(1)}, f32[1,512]{1,0:T(1,128)}, u32[]{:S(2)}) copy-start(f32[1,512]{1,0:T(1,128)} %get-tuple-element.203) | copy-start | bytes 6148
  258.5 75.3 %copy-start.190 = (f32[1,512]{1,0:T(1,128)S(1)}, f32[1,512]{1,0:T(1,128)}, u32[]{:S(2)}) copy-start(f32[1,512]{1,0:T(1,128)} %get-tuple-element.202) | copy-start | bytes 6148
  258.5 75.4 %copy-start.187 = (f32[1,512]{1,0:T(1,128)S(1)}, f32[1,512]{1,0:T(1,128)}, u32[]{:S(2)}) copy-start(f32[1,512]{1,0:T(1,128)} %get-tuple-element.201) | copy-start | bytes 6148
  258.5 75.4 %copy-start.183 = (f32[1,512]{1,0:T(1,128)S(1)}, f32[1,512]{1,0:T(1,128)}, u32[]{:S(2)}) copy-start(f32[1,512]{1,0:T(1,128)} %get-tuple-element.200) | copy-start | bytes 6148
  258.6 75.5 %copy-start.178 = (f32[1,512]{1,0:T(1,128)S(1)}, f32[1,512]{1,0:T(1,128)}, u32[]{:S(2)}) copy-start(f32[1,512]{1,0:T(1,128)} %get-tuple-element.199) | copy-start | bytes 6148
  (181 other events, 542.3 us)
Sparse Core Ops, SparseCore 0:
  248.0 82.0 reduce-scatter.1
where the time goes:
time: 347 us; the launch traced here: 346 us
  waiting for transfers between devices  193 us (56%)
  local copies, waits for them, and re-layouts  35.9 us (10%)
  matrix products  34.4 us (10%)
  other arithmetic  26.4 us (8%)
  starting transfers between devices  19.5 us (6%)
  blocking collectives  19.2 us (6%)
  between operations  17.8 us (5%)
    all_to_all x1, waiting for transfers between devices, shards(): lax.all_to_all(picked.reshape(group_count, capacity, coef_count * local_c...  114 us
    reduce_scatter x1, waiting for transfers between devices, shards(): lax.psum_scatter(convolve(turned, weight_zero, weight_one, weight_two, mi...  71.5 us
    dot_general x9, matrix products, mixed_contract(): jnp.einsum(pattern, first_operand, second_operand, preferred_element_type...  14.5 us
    concatenate x1, local copies, waits for them, and re-layouts, convolve(): jnp.concatenate([out_zero, out_one_plus, out_one_minus, out_two_plus, out...  14.5 us
    all_to_all x1, starting transfers between devices, shards(): lax.all_to_all(requests, 'edge', split_axis=0, concat_axis=0, tiled=True)  13.6 us
    all_gather x1, blocking collectives, shards(): lax.all_gather(quarter.astype(jnp.bfloat16), 'chan', axis=0, tiled=True)  9.89 us
    all_gather x1, blocking collectives, shards(): lax.all_gather(quarter_fade.astype(jnp.bfloat16), 'chan', axis=0, tiled=T...  9.35 us
    convert_element_type x1, local copies, waits for them, and re-layouts, pick_rows(): jnp.dot(selector, table, preferred_element_type=jnp.float32)  9.26 us
  transfers between devices with their start and end apart: 3, of which 3 were waited for; matrix products, arithmetic and copies ran while one was open for 6% of the time, Pallas kernels for 0%

commit v1 on v0

--- a/solution.py
+++ b/solution.py
@@ -117,37 +117,25 @@
     return (compact, envelope)
 
 
-def rotate_forward(compact_t, sources):
+def one_hot(indices, width):
+    return (indices[:, None] == jnp.arange(width, dtype=jnp.int32)[None, :]).astype(jnp.bfloat16)
+
+
+def rotate_forward(compact_t, scaling, sources):
     rows_out = []
     for degree, offset in row_offsets():
-        total = compact_t[offset].astype(jnp.float32)[None, :] * sources[degree * degree].astype(
-            jnp.float32
-        )
-        for inner in range(1, 2 * degree + 1):
-            total = total + compact_t[offset + inner].astype(jnp.float32)[None, :] * sources[
+        span = 2 * degree + 1
+        total = None
+        for inner in range(span):
+            term = compact_t[offset + inner].astype(jnp.float32)[None, :] * sources[
                 degree * degree + inner
             ].astype(jnp.float32)
-        rows_out.append(total)
+            total = term if total is None else total + term
+        rows_out.append(total * scaling[None, :])
     return jnp.stack(rows_out, axis=0).astype(jnp.bfloat16)
 
 
-def rotate_back(compact_t, scaled):
-    listing = row_offsets()
-    coefs_out = []
-    for degree in range(LMAX + 1):
-        for inner in range(2 * degree + 1):
-            total = None
-            for row_index, (row_degree, offset) in enumerate(listing):
-                if row_degree == degree:
-                    term = compact_t[offset + inner].astype(jnp.float32)[None, :] * scaled[
-                        :, row_index
-                    ].astype(jnp.float32)
-                    total = term if total is None else total + term
-            coefs_out.append(total)
-    return jnp.stack(coefs_out, axis=0).astype(jnp.bfloat16)
-
-
-def convolve(turned, weight_zero, weight_one, weight_two, contract):
+def convolve(turned, weight_zero, weight_one, weight_two):
     end_zero = LMAX + 1
     end_one_plus = end_zero + LMAX
     end_one_minus = end_one_plus + LMAX
@@ -157,42 +145,24 @@
     one_minus = turned[end_one_plus:end_one_minus]
     two_plus = turned[end_one_minus:end_two_plus]
     two_minus = turned[end_two_plus:]
-    pattern = "lce,lcjd->dje"
-    out_zero = contract(pattern, zero_part, weight_zero)
-    out_one_plus = contract(pattern, one_plus, weight_one[0]) - contract(
-        pattern, one_minus, weight_one[1]
-    )
-    out_one_minus = contract(pattern, one_minus, weight_one[0]) + contract(
-        pattern, one_plus, weight_one[1]
-    )
-    out_two_plus = contract(pattern, two_plus, weight_two[0]) - contract(
-        pattern, two_minus, weight_two[1]
-    )
-    out_two_minus = contract(pattern, two_minus, weight_two[0]) + contract(
-        pattern, two_plus, weight_two[1]
-    )
-    return jnp.concatenate(
-        [out_zero, out_one_plus, out_one_minus, out_two_plus, out_two_minus], axis=1
-    )
-
-
-def mixed_contract(pattern, first_operand, second_operand):
-    return jnp.einsum(pattern, first_operand, second_operand, preferred_element_type=jnp.float32)
-
-
-def one_hot(indices, width):
-    return (indices[:, None] == jnp.arange(width, dtype=jnp.int32)[None, :]).astype(jnp.bfloat16)
-
-
-def pick_columns(table, selector):
-    picked = lax.dot_general(
-        table, selector, (((0,), (1,)), ((), ())), preferred_element_type=jnp.float32
-    )
-    return picked.astype(jnp.bfloat16)
-
-
-def pick_rows(selector, table):
-    return jnp.dot(selector, table, preferred_element_type=jnp.float32).astype(jnp.bfloat16)
+
+    def contract(parts, weight, rows):
+        left = jnp.concatenate(parts, axis=0)
+        edges = left.shape[-1]
+        left = left.reshape(-1, edges)
+        right = weight.reshape(left.shape[0], -1)
+        out = lax.dot_general(
+            left, right, (((0,), (0,)), ((), ())), preferred_element_type=jnp.float32
+        ).astype(jnp.bfloat16)
+        return [out[:, row * 256 : (row + 1) * 256] for row in range(rows)]
+
+    return (
+        contract([zero_part], weight_zero, LMAX + 1)
+        + contract([one_plus, -one_minus], weight_one, LMAX)
+        + contract([one_minus, one_plus], weight_one, LMAX)
+        + contract([two_plus, -two_minus], weight_two, LMAX - 1)
+        + contract([two_minus, two_plus], weight_two, LMAX - 1)
+    )
 
 
 def shards(
@@ -211,58 +181,52 @@
     local_channels = node_states.shape[2]
     coef_count = node_states.shape[1]
     group_count = lax.axis_size("edge")
-    capacity = max(2, 2 * slab_size // group_count)
-    slot_total = group_count * capacity
+    node_flat = node_states.reshape(local_nodes, coef_count * local_channels)
+    table = lax.all_gather(node_flat, "edge", axis=0, tiled=True)
     quarter, quarter_fade = wigner_rows(edge_vectors)
-    compact, envelope = (
-        lax.all_gather(quarter.astype(jnp.bfloat16), "chan", axis=0, tiled=True),
-        lax.all_gather(quarter_fade.astype(jnp.bfloat16), "chan", axis=0, tiled=True),
-    )
-    compact_t = compact.T
-    node_flat = node_states.reshape(local_nodes, coef_count * local_channels)
-    owner_part = source_part[:, 0]
-    owners = jnp.arange(group_count, dtype=jnp.int32)
-    member = (owner_part[:, None] == owners[None, :]).astype(jnp.int32)
-    earlier = jnp.cumsum(member, axis=0) - member
-    position = jnp.sum(earlier * member, axis=1)
-    slot_flat = owner_part * capacity + position
-    requests = (
-        jnp.zeros((slot_total,), jnp.int32)
-        .at[slot_flat]
-        .set(source_slot)
-        .reshape(group_count, capacity)
-    )
-    slot_select = one_hot(slot_flat, slot_total)
-    wanted = lax.all_to_all(requests, "edge", split_axis=0, concat_axis=0, tiled=True)
-    picked = pick_rows(one_hot(wanted.reshape(-1), local_nodes), node_flat)
-    returned = lax.all_to_all(
-        picked.reshape(group_count, capacity, coef_count * local_channels),
-        "edge",
-        split_axis=0,
-        concat_axis=0,
-        tiled=True,
-    )
-    sources = pick_columns(
-        returned.reshape(slot_total, coef_count * local_channels), slot_select
-    ).reshape(coef_count, local_channels, slab_size)
-    turned = rotate_forward(compact_t, sources)
-    channel_mix = lax.psum_scatter(
-        convolve(turned, weight_zero, weight_one, weight_two, mixed_contract).astype(jnp.bfloat16),
-        "chan",
-        scatter_dimension=0,
-        tiled=True,
-    ).astype(jnp.float32)
+    packed = jnp.concatenate([quarter, quarter_fade[:, None]], axis=1).astype(jnp.bfloat16)
+    packed_t = lax.all_gather(packed, "chan", axis=0, tiled=True).T
+    compact_t, envelope = packed_t[:-1], packed_t[-1]
     alive_mask = (jnp.arange(slab_size, dtype=jnp.int32) < live_edges[0]).astype(jnp.float32)
     scaling = envelope.astype(jnp.float32) * alive_mask
-    scaled = (channel_mix * scaling).astype(jnp.bfloat16)
-    message = rotate_back(compact_t, scaled).reshape(coef_count * local_channels, slab_size)
+    source = source_part[:, 0] * local_nodes + source_slot
+    select = one_hot(source, group_count * local_nodes)
+    sources = (
+        lax.dot_general(
+            table, select, (((0,), (1,)), ((), ())), preferred_element_type=jnp.float32
+        )
+        .astype(jnp.bfloat16)
+        .reshape(coef_count, local_channels, slab_size)
+    )
+    turned = rotate_forward(compact_t, scaling, sources)
+    mixed = convolve(turned, weight_zero, weight_one, weight_two)
     selector = (jnp.arange(local_nodes, dtype=jnp.int32)[:, None] == target_slot[None, :]).astype(
         jnp.bfloat16
     )
-    summed = lax.dot_general(
-        selector, message, (((1,), (1,)), ((), ())), preferred_element_type=jnp.float32
-    )
-    return summed.astype(jnp.bfloat16).reshape(local_nodes, coef_count, local_channels)
+    listing = row_offsets()
+    sums = []
+    for degree in range(LMAX + 1):
+        span = 2 * degree + 1
+        picked_rows = [
+            (row, offset) for row, (row_degree, offset) in enumerate(listing) if row_degree == degree
+        ]
+        left = jnp.concatenate(
+            [
+                (compact_t[offset : offset + span][None] * selector[:, None]).reshape(
+                    local_nodes * span, slab_size
+                )
+                for row, offset in picked_rows
+            ],
+            axis=1,
+        )
+        right = jnp.concatenate([mixed[row] for row, offset in picked_rows], axis=0)
+        sums.append(
+            jnp.dot(left, right, preferred_element_type=jnp.float32).reshape(
+                local_nodes, span, -1
+            )
+        )
+    partial = jnp.concatenate(sums, axis=1).astype(jnp.bfloat16)
+    return lax.psum_scatter(partial, "chan", scatter_dimension=2, tiled=True)
 
 
 def solution(mesh):

time: 347 us -> 410 us (1.18)
  waiting for transfers between devices: 193 us -> 247 us
  local copies, waits for them, and re-layouts: 35.9 us -> 75.8 us
  starting transfers between devices: 19.5 us -> 0.04 us
  blocking collectives: 19.2 us -> 10.5 us
    all_gather x0 -> x1, waiting for transfers between devices: none -> 173 us  [shards(): table = lax.all_gather(node_flat, 'edge', axis=0, tiled=True)]
    all_to_all x2 -> x0, waiting for transfers between devices: 121 us -> none  [the longest x1 114 us: shards(): lax.all_to_all(picked.reshape(group_count, capacity, coef_count * local_c...]
    unnamed x1 -> x3, waiting for transfers between devices: 0.02 us -> 73.7 us
    reduce_scatter x1 -> x0, waiting for transfers between devices: 71.5 us -> none  [shards(): lax.psum_scatter(convolve(turned, weight_zero, weight_one, weight_two, mi...]
    unnamed x421 -> x534, local copies, waits for them, and re-layouts: 2.38 us -> 36.1 us
    mul x0 -> x28, local copies, waits for them, and re-layouts: none -> 30.4 us  [shards(): compact_t[offset:offset + span][None] * selector[:, None]]
    all_to_all x2 -> x0, starting transfers between devices: 19.4 us -> none  [the longest x1 13.6 us: shards(): lax.all_to_all(requests, 'edge', split_axis=0, concat_axis=0, tiled=True)]
    concatenate x2 -> x9, local copies, waits for them, and re-layouts: 16.6 us -> 5.4 us  [the longest x5 2.34 us: shards(): jnp.concatenate([(compact_t[offset:offset + span][None] * selector[:, Non...]
  transfers between devices with their start and end apart: 3 -> 2, of which waited for: 3 -> 2; matrix products, arithmetic and copies ran while one was open for 6% -> 20% of each run, Pallas kernels for 0% -> 0%
where the time goes in v1:
time: 410 us; the launch traced here: 409 us
  waiting for transfers between devices  247 us (60%)
  local copies, waits for them, and re-layouts  75.8 us (18%)
  matrix products  30.5 us (7%)
  other arithmetic  26.9 us (7%)
  between operations  18.1 us (4%)
  blocking collectives  10.5 us (3%)
    all_gather x1, waiting for transfers between devices, shards(): table = lax.all_gather(node_flat, 'edge', axis=0, tiled=True)  173 us
    unnamed x3, waiting for transfers between devices  73.7 us
    unnamed x534, local copies, waits for them, and re-layouts  36.1 us
    mul x28, local copies, waits for them, and re-layouts, shards(): compact_t[offset:offset + span][None] * selector[:, None]  30.4 us
    all_gather x1, blocking collectives, shards(): packed_t = lax.all_gather(packed, 'chan', axis=0, tiled=True).T  10.5 us
    mul x14, other arithmetic, rotate_forward(): compact_t[offset + inner].astype(jnp.float32)[None, :]  9.2 us
    dot_general x1, matrix products, shards(): lax.dot_general(table, select, (((0,), (1,)), ((), ())), preferred_elemen...  8.62 us
  transfers between devices with their start and end apart: 2, of which 2 were waited for; matrix products, arithmetic and copies ran while one was open for 20% of the time, Pallas kernels for 0%

profile of v1, /device:TPU:1, one launch (start us, length us, event | category | flops | bytes accessed | tf_op | source)
XLA Modules:
  0.0 408.8 jit_solution(11529215945910362788)
XLA Ops:
  20.3 2.1 concatenate.68
  22.4 10.5 %all_gather.6 = bf16[512,236]{0,1:T(8,128)(2,1)S(1)} all-gather(bf16[128,236]{0,1:T(8,128)(2,1)S(1)} %concatenate.68), channel_id=1, replica_groups=mesh['edge'=64,'chan'=4] {'chan'}, dimensions={0}, use_global_device_ids=true | all-gather | bytes 302080 | tf_op jit(solution)/shard_map/all_gather | solution.py:188
  35.3 1.8 copy.63
  37.2 1.7 copy.54
  41.3 1.7 copy.61
  44.0 1.7 mul.5643
  45.7 1.7 mul.5646
  50.6 1.7 mul.5627
  52.3 1.7 mul.5630
  57.2 1.7 mul.5611
  58.9 1.7 mul.5614
  61.6 1.6 mul.5595
  63.2 1.6 mul.5598
  64.8 1.6 mul.5601
  67.3 1.6 mul.5199
  68.9 1.6 mul.5202
  70.5 1.6 mul.5205
  74.1 1.5 mul.4781
  75.6 1.5 mul.4784
  77.1 1.5 mul.4787
  85.1 1.7 constant_dynamic-update-slice_fusion.60
  86.8 1.5 constant_dynamic-update-slice_fusion.59
  104.1 173.3 %all-gather.2.cloned.1.call-done = bf16[1024,3136]{1,0:T(8,128)(2,1)} async-done(((bf16[16,3136]{1,0:T(8,128)(2,1)}), bf16[1024,3136]{1,0:T(8,128)(2,1)}) %all-gather.2.cloned.1.call-update) | async-done | bytes 6422544 | tf_op jit(solution)/shard_map/all_gather | solution.py:185
  277.4 8.6 %fusion = bf16[3136,512]{1,0:T(8,128)(2,1)S(1)} fusion(bf16[1024,3136]{1,0:T(8,128)(2,1)} %all-gather.2.cloned.1.call-done, s32[512]{0:T(512)} %add.1082), kind=kOutput, calls=%fused_computation.1 | convolution fusion | flops 3290464256 | bytes 9635840 | tf_op jit(solution)/shard_map/dot_general | solution.py:195
  300.0 1.4 convolution_convert_fusion.3
  301.7 1.4 convolution_convert_fusion.4
  312.5 2.0 convolution_convert_fusion.6
  317.3 1.5 convolution_convert_fusion.8
  318.9 1.5 convolution_convert_fusion.9
  323.8 2.1 reshape.3360
  325.8 73.7 %reduce-scatter.4.cloned.1.call-done = bf16[64,784]{1,0:T(8,128)(2,1)} async-done(((bf16[256,784]{1,0:T(8,128)(2,1)}), bf16[64,784]{1,0:T(8,128)(2,1)}) %reduce-scatter.4.cloned.1.call-update) | async-done | bytes 100368
  399.6 1.3 reshape.3361
  (672 shorter events, 78.7 us)
Async XLA Ops:
  6.5 6.0 %copy-start.34 = (f32[98,7]{1,0:T(8,128)S(1)}, f32[98,7]{1,0:T(8,128)}, u32[]{:S(2)}) copy-start(f32[98,7]{1,0:T(8,128)} %constant.140.clone) | copy-start | bytes 8236
  6.5 6.5 %copy-start.13 = (f32[98,5]{1,0:T(8,128)S(1)}, f32[98,5]{1,0:T(8,128)}, u32[]{:S(2)}) copy-start(f32[98,5]{1,0:T(8,128)} %constant.139.clone) | copy-start | bytes 5884
  6.5 7.5 %copy-start.29 = (f32[98,3]{1,0:T(8,128)S(1)}, f32[98,3]{1,0:T(8,128)}, u32[]{:S(2)}) copy-start(f32[98,3]{1,0:T(8,128)} %constant.138.clone) | copy-start | bytes 3532
  6.5 270.9 %all-gather.2.cloned.1.call-start = ((), (), s32[]{:S(2)}) async-start(), calls=%async_computation.1 | async-start | bytes 6656000 | tf_op jit(solution)/shard_map/all_gather | solution.py:185
  8.4 6.9 %copy-start.240 = (f32[98,13]{1,0:T(8,128)S(1)}, f32[98,13]{1,0:T(8,128)}, u32[]{:S(2)}) copy-start(f32[98,13]{1,0:T(8,128)} %constant.143.clone) | copy-start | bytes 15292
  8.4 391.1 %reduce-scatter.4.cloned.1.call-start = ((), (), s32[]{:S(2)}) async-start(), calls=%async_computation.2 | async-start | bytes 573440
  12.5 3.0 copy-start.239
  12.5 3.2 copy-start.238
  18.6 15.5 %copy-start.9 = (bf16[2,5,64,5,256]{4,2,3,1,0:T(8,128)(2,1)S(1)}, bf16[2,5,64,5,256]{4,2,3,1,0:T(8,128)(2,1)}, u32[]{:S(2)}) copy-start(bf16[2,5,64,5,256]{4,2,3,1,0:T(8,128)(2,1)} %param.49) | copy-start | bytes 4915204
  72.7 15.7 %copy-start.30 = (bf16[112,512]{1,0:T(8,128)(2,1)S(1)}, bf16[112,512]{1,0:T(8,128)(2,1)}, u32[]{:S(2)}) copy-start(bf16[112,512]{1,0:T(8,128)(2,1)} %mul.5601) | copy-start | bytes 344068
  73.4 17.0 %copy-start.27 = (bf16[144,512]{1,0:T(8,128)(2,1)S(1)}, bf16[144,512]{1,0:T(8,128)(2,1)}, u32[]{:S(2)}) copy-start(bf16[144,512]{1,0:T(8,128)(2,1)} %mul.5611) | copy-start | bytes 442372
  85.1 4.7 %copy-start.25 = (bf16[80,2560]{1,0:T(8,128)(2,1)}, bf16[80,2560]{1,0:T(8,128)(2,1)S(1)}, u32[]{:S(2)}) copy-start(bf16[80,2560]{1,0:T(8,128)(2,1)S(1)} %constant_dynamic-update-slice_fusion.31) | copy-start | bytes 1228804
  85.1 6.4 %copy-start.23 = (bf16[176,512]{1,0:T(8,128)(2,1)S(1)}, bf16[176,512]{1,0:T(8,128)(2,1)}, u32[]{:S(2)}) copy-start(bf16[176,512]{1,0:T(8,128)(2,1)} %mul.5627) | copy-start | bytes 540676
  88.4 3.2 copy-start.24
  89.0 2.5 copy-start.22
  91.5 4.5 %copy-start.14 = (bf16[144,2560]{1,0:T(8,128)(2,1)}, bf16[144,2560]{1,0:T(8,128)(2,1)S(1)}, u32[]{:S(2)}) copy-start(bf16[144,2560]{1,0:T(8,128)(2,1)S(1)} %constant_dynamic-update-slice_fusion.61) | copy-start | bytes 2211844
  91.5 3.0 copy-start.15
  91.6 3.7 copy-start.16
  104.0 182.1 %copy-start.185 = (f32[1,512]{1,0:T(1,128)S(1)}, f32[1,512]{1,0:T(1,128)}, u32[]{:S(2)}) copy-start(f32[1,512]{1,0:T(1,128)} %get-tuple-element.152) | copy-start | bytes 6148
  104.0 182.1 %copy-start.186 = (f32[1,512]{1,0:T(1,128)S(1)}, f32[1,512]{1,0:T(1,128)}, u32[]{:S(2)}) copy-start(f32[1,512]{1,0:T(1,128)} %get-tuple-element.153) | copy-start | bytes 6148
  104.0 182.1 %copy-start.187 = (f32[1,512]{1,0:T(1,128)S(1)}, f32[1,512]{1,0:T(1,128)}, u32[]{:S(2)}) copy-start(f32[1,512]{1,0:T(1,128)} %get-tuple-element.154) | copy-start | bytes 6148
  104.0 182.1 %copy-start.188 = (f32[1,512]{1,0:T(1,128)S(1)}, f32[1,512]{1,0:T(1,128)}, u32[]{:S(2)}) copy-start(f32[1,512]{1,0:T(1,128)} %get-tuple-element.155) | copy-start | bytes 6148
  104.0 182.1 %copy-start.189 = (f32[1,512]{1,0:T(1,128)S(1)}, f32[1,512]{1,0:T(1,128)}, u32[]{:S(2)}) copy-start(f32[1,512]{1,0:T(1,128)} %get-tuple-element.156) | copy-start | bytes 6148
  104.0 182.4 %copy-start.162 = (f32[1,512]{1,0:T(1,128)S(1)}, f32[1,512]{1,0:T(1,128)}, u32[]{:S(2)}) copy-start(f32[1,512]{1,0:T(1,128)} %get-tuple-element.148) | copy-start | bytes 6148
  104.1 182.4 %copy-start.163 = (f32[1,512]{1,0:T(1,128)S(1)}, f32[1,512]{1,0:T(1,128)}, u32[]{:S(2)}) copy-start(f32[1,512]{1,0:T(1,128)} %get-tuple-element.149) | copy-start | bytes 6148
  104.1 182.4 %copy-start.164 = (f32[1,512]{1,0:T(1,128)S(1)}, f32[1,512]{1,0:T(1,128)}, u32[]{:S(2)}) copy-start(f32[1,512]{1,0:T(1,128)} %get-tuple-element.150) | copy-start | bytes 6148
  104.1 182.4 %copy-start.165 = (f32[1,512]{1,0:T(1,128)S(1)}, f32[1,512]{1,0:T(1,128)}, u32[]{:S(2)}) copy-start(f32[1,512]{1,0:T(1,128)} %get-tuple-element.151) | copy-start | bytes 6148
  277.4 9.1 %copy-start.197 = (f32[1,512]{1,0:T(1,128)S(1)}, f32[1,512]{1,0:T(1,128)}, u32[]{:S(2)}) copy-start(f32[1,512]{1,0:T(1,128)} %get-tuple-element.144) | copy-start | bytes 6148
  277.4 9.1 %copy-start.198 = (f32[1,512]{1,0:T(1,128)S(1)}, f32[1,512]{1,0:T(1,128)}, u32[]{:S(2)}) copy-start(f32[1,512]{1,0:T(1,128)} %get-tuple-element.145) | copy-start | bytes 6148
  277.4 9.1 %copy-start.199 = (f32[1,512]{1,0:T(1,128)S(1)}, f32[1,512]{1,0:T(1,128)}, u32[]{:S(2)}) copy-start(f32[1,512]{1,0:T(1,128)} %get-tuple-element.146) | copy-start | bytes 6148
  312.5 2.8 copy-start.2
  316.3 2.6 copy-start.8
  (211 other events, 334.5 us)
Sparse Core Ops, SparseCore 0:
  9.1 268.2 all-gather.1
  326.0 73.5 reduce-scatter.3

commit v2 on v1

v2 whole, which is shorter than its diff:
```python
import math

import jax
import jax.numpy as jnp
import numpy as np
from jax import lax
from jax.experimental import pallas as pl
from jax.experimental.pallas import tpu as pltpu
from jax.sharding import PartitionSpec as P

LMAX = 6
MMAX = 2
COEFS = (LMAX + 1) ** 2
CUTOFF = 6.0
LANES = 128
MESH = pl.DeviceIdType.MESH

Y_RING, Z_RING = 4, 8
HALVES = {"A": ((0, 5), (5, 10)), "B": ((10, 18), (18, 25))}


def schedule():
    step = {"y+": (1, 0), "y-": (-1, 0), "z+": (0, 1), "z-": (0, -1)}
    free = {link: 0.0 for link in step}
    waiting = {link: [] for link in step}
    events = [(4.0, 0, "A", (0, 1), 0, 0, ""), (4.0, 1, "B", (0, 1), 0, 0, "")]
    count = 2
    sends = []

    def follow(colour, half, oy, oz, via):
        first, second = ("y", "z") if colour == "A" else ("z", "y")
        offset = {"y": oy, "z": oz}
        limit = {"y": Y_RING // 2, "z": Z_RING // 2}
        routes = []

        def along(axis, rank):
            moved = offset[axis]
            for sign, mine in (("+", 0), ("-", 1)):
                if moved != 0 and via != axis + sign:
                    continue
                hops = abs(moved) + 1
                if hops > limit[axis]:
                    continue
                taken = (mine,) if hops == limit[axis] else half
                taken = tuple(h for h in taken if h in half)
                if taken:
                    routes.append((rank + limit[axis] - hops, axis + sign, taken))

        if offset[second] == 0:
            along(first, 10)
        along(second, 0)
        return routes

    while events or any(waiting.values()):
        ready = [
            (max(free[link], min(item[0] for item in items)), link)
            for link, items in waiting.items()
            if items
        ]
        begin = min(ready) if ready else None
        if events and (begin is None or min(events)[0] <= begin[0]):
            event = min(events)
            events.remove(event)
            time, _, colour, half, oy, oz, via = event
            for rank, link, taken in follow(colour, half, oy, oz, via):
                waiting[link].append((time, -rank, count, colour, taken, oy, oz))
                count += 1
            continue
        time, link = begin
        items = [item for item in waiting[link] if item[0] <= time]
        item = min(items, key=lambda it: (it[1], it[0], it[2]))
        waiting[link].remove(item)
        _, _, _, colour, half, oy, oz = item
        tiles = [HALVES[colour][h] for h in half]
        first, end = tiles[0][0], tiles[-1][1]
        free[link] = time + (end - first) * 2 * 4096 / 46.6e3
        dy, dz = step[link]
        sends.append((time, link, first, end, oy, oz))
        events.append((free[link] + 1.8, count, colour, half, oy - dy, oz - dz, link))
        count += 1
    return [send[1:] for send in sorted(sends)]


SENDS = schedule()
STEP = {"y+": (1, 0), "y-": (-1, 0), "z+": (0, 1), "z-": (0, -1)}
TILES = 25


def harmonics_at(points, degree_top):
    x, y, z = points
    rows = {}
    real, imag = [np.ones_like(x)], [np.zeros_like(x)]
    for m in range(1, degree_top + 1):
        real.append(x * real[m - 1] - y * imag[m - 1])
        imag.append(x * imag[m - 1] + y * real[m - 1])
    for m in range(degree_top + 1):
        start = (-1.0) ** m * math.prod(range(2 * m - 1, 0, -2))
        legendre = {m: np.full_like(z, start), m + 1: z * ((2 * m + 1) * start)}
        for l in range(m + 2, degree_top + 1):
            legendre[l] = (
                (2 * l - 1) * z * legendre[l - 1] - (l + m - 1) * legendre[l - 2]
            ) / (l - m)
        for l in range(m, degree_top + 1):
            factor = math.sqrt(
                (2 * l + 1) / (4 * math.pi) * math.factorial(l - m) / math.factorial(l + m)
            )
            if m == 0:
                rows[l, 0] = factor * legendre[l]
            else:
                rows[l, m] = math.sqrt(2.0) * factor * legendre[l] * real[m]
                rows[l, -m] = math.sqrt(2.0) * factor * legendre[l] * imag[m]
    return np.stack([rows[l, m] for l in range(degree_top + 1) for m in range(-l, l + 1)])


def raising_tables():
    count = 4 * (LMAX + 2) ** 2
    at = np.arange(count) + 0.5
    height = 1.0 - 2.0 * at / count
    radius = np.sqrt(1.0 - height * height)
    angle = math.pi * (3.0 - math.sqrt(5.0)) * at
    points = np.stack([radius * np.cos(angle), radius * np.sin(angle), height])
    basis = harmonics_at(points, LMAX)
    inverse = np.linalg.pinv(basis.T)
    tables = {}
    for l in range(1, LMAX + 1):
        below = basis[(l - 1) ** 2 : l * l]
        tables[l] = [
            np.where(np.abs(part) < 1e-9, 0.0, part)
            for part in (
                (inverse @ (points[c] * below).T)[l * l : (l + 1) ** 2] for c in range(3)
            )
        ]
    return tables


RAISE = raising_tables()


def project(table, degree, weights, rows):
    results = []
    for m in range(2 * degree + 1):
        total = None
        for axis in range(3):
            for n in range(2 * degree - 1):
                value = float(table[axis][m, n])
                if value != 0.0:
                    term = (value * weights[axis]) * rows[n]
                    total = term if total is None else total + term
        results.append(total)
    return results


def wigner_into(rot_ref, vectors):
    x, y, z = vectors[0:1], vectors[1:2], vectors[2:3]
    length = jnp.sqrt(x * x + y * y + z * z)
    u = [x / length, y / length, z / length]
    pick = jnp.where(jnp.abs(u[0]) < 0.6, 1.0, 0.0)
    other = 1.0 - pick
    a = [-u[2] * other, u[2] * pick, u[0] * other - u[1] * pick]
    norm = jnp.sqrt(a[0] * a[0] + a[1] * a[1] + a[2] * a[2])
    a = [part / norm for part in a]
    b = [
        u[1] * a[2] - u[2] * a[1],
        u[2] * a[0] - u[0] * a[2],
        u[0] * a[1] - u[1] * a[0],
    ]
    shape = (8, x.shape[1])
    order = lax.broadcasted_iota(jnp.int32, shape, 0)
    wide = [jnp.broadcast_to(part, shape) for part in u]
    below = [jnp.where(order == 0, 1.0, 0.0)]
    rot_ref[0] = below[0]
    for l in range(1, LMAX + 1):
        table = RAISE[l]
        inverse = [1.0 / float(table[2][m + l, m + l - 1]) if m < l else 0.0 for m in range(3)]
        scale = jnp.where(
            order == 0, inverse[0], jnp.where(order <= 2, inverse[1], inverse[2])
        )
        rows = project(table, l, [part * scale for part in wide], below)
        rows = [jnp.zeros(shape, jnp.float32) if row is None else row for row in rows]
        if l == 1:
            first = project(table, 1, a, [1.0])
            second = project(table, 1, b, [1.0])
            one = 1.0 / float(table[0][2, 0])
            two = 1.0 / float(table[1][0, 0])
            rows = [
                jnp.where(order == 1, one * f, jnp.where(order == 2, two * s, r))
                for f, s, r in zip(first, second, rows)
            ]
        if l == 2:
            plus = [row[1:2] for row in below]
            minus = [row[2:3] for row in below]
            aa, bb = project(table, 2, a, plus), project(table, 2, b, minus)
            ab, ba = project(table, 2, a, minus), project(table, 2, b, plus)
            one = 1.0 / float(table[0][4, 2] - table[1][4, 0])
            two = 1.0 / float(table[0][0, 0] + table[1][0, 2])
            rows = [
                jnp.where(
                    order == 3,
                    one * (aa[m] - bb[m]),
                    jnp.where(order == 4, two * (ab[m] + ba[m]), rows[m]),
                )
                for m in range(5)
            ]
        for k, row in enumerate(rows):
            rot_ref[l * l + k] = row
        below = rows
    return length


def gather_kernel(block_ref, vector_ref, table_ref, vectors_ref, send, recv, xsem, vsem, own):
    edge = lax.axis_index("edge")
    chan = lax.axis_index("chan")
    x = edge % 2
    z = (edge // 2) % Z_RING
    y = edge // (2 * Z_RING)

    def at(oy, oz, side=0):
        row = (y + (oy + Y_RING)) % Y_RING
        column = (z + (oz + Z_RING)) % Z_RING
        return (row * Z_RING + column) * 2 + side

    partner = at(0, 0, 1 - x)
    neighbours = {link: at(dy, dz, x) for link, (dy, dz) in STEP.items()}
    barrier = pltpu.get_barrier_semaphore()
    for target in [partner, *neighbours.values()]:
        pl.semaphore_signal(
            barrier, inc=1, device_id={"edge": target, "chan": chan}, device_id_type=MESH
        )
    for far in range(1, 4):
        pl.semaphore_signal(
            barrier,
            inc=1,
            device_id={"edge": edge, "chan": (chan + far) % 4},
            device_id_type=MESH,
        )
    mine = pltpu.make_async_copy(block_ref, table_ref.at[edge], own.at[0])
    mine.start()
    vector = pltpu.make_async_copy(vector_ref, vectors_ref.at[chan], own.at[1])
    vector.start()
    pl.semaphore_wait(barrier, 8)
    across = pltpu.make_async_remote_copy(
        src_ref=block_ref,
        dst_ref=table_ref.at[edge],
        send_sem=xsem.at[0],
        recv_sem=xsem.at[1],
        device_id={"edge": partner, "chan": chan},
        device_id_type=MESH,
    )
    across.start()
    spread = []
    for far in range(1, 4):
        copy = pltpu.make_async_remote_copy(
            src_ref=vector_ref,
            dst_ref=vectors_ref.at[chan],
            send_sem=vsem.at[far - 1],
            recv_sem=vsem.at[far + 2],
            device_id={"edge": edge, "chan": (chan + far) % 4},
            device_id_type=MESH,
        )
        copy.start()
        spread.append(copy)
    mine.wait()
    vector.wait()
    across.wait_recv()
    copies, landed = [], []
    for index, (link, first, end, oy, oz) in enumerate(SENDS):
        dy, dz = STEP[link]
        view = table_ref.at[pl.ds(at(oy, oz), 2), pl.ds(first, end - first)]
        copies.append(
            pltpu.make_async_remote_copy(
                src_ref=view,
                dst_ref=view,
                send_sem=send.at[index],
                recv_sem=recv.at[index],
                device_id={"edge": neighbours[link], "chan": chan},
                device_id_type=MESH,
            )
        )
        landed.append((first, end, (oy - dy) % Y_RING, (oz - dz) % Z_RING))
    waited = set()
    for index, (link, first, end, oy, oz) in enumerate(SENDS):
        for other, (begin, stop, ry, rz) in enumerate(landed):
            if (
                other not in waited
                and (ry, rz) == (oy % Y_RING, oz % Z_RING)
                and begin < end
                and first < stop
            ):
                copies[other].wait_recv()
                waited.add(other)
        copies[index].start()
    for index, copy in enumerate(copies):
        if index not in waited:
            copy.wait_recv()
    for copy in spread:
        copy.wait()
    across.wait_send()
    for copy in copies:
        copy.wait_send()


def gather(block, vector):
    return pl.pallas_call(
        gather_kernel,
        name="gather_table",
        out_shape=(
            jax.ShapeDtypeStruct((64, *block.shape), block.dtype),
            jax.ShapeDtypeStruct((4, *vector.shape), vector.dtype),
        ),
        in_specs=[pl.BlockSpec(memory_space=pltpu.VMEM)] * 2,
        out_specs=[pl.BlockSpec(memory_space=pltpu.VMEM)] * 2,
        scratch_shapes=[
            pltpu.SemaphoreType.DMA((len(SENDS),)),
            pltpu.SemaphoreType.DMA((len(SENDS),)),
            pltpu.SemaphoreType.DMA((2,)),
            pltpu.SemaphoreType.DMA((6,)),
            pltpu.SemaphoreType.DMA((2,)),
        ],
        compiler_params=pltpu.CompilerParams(
            collective_id=0, has_side_effects=True, vmem_limit_bytes=40 << 20
        ),
    )(block, vector)


STARTS = {"p1": 0, "n1": 768, "p2": 1536, "n2": 2176, "z": 2816}
LEFT_BLOCKS = 26


def left_rows(order, degree):
    if order == 0:
        return [(STARTS["z"] + 64 * degree, False)]
    m = (order + 1) // 2
    count = LMAX + 1 - m
    plus, minus = STARTS["p%d" % m], STARTS["n%d" % m]
    here = 64 * (degree - m)
    if order % 2:
        return [(plus + here, False), (minus + 64 * count + here, False)]
    return [(minus + here, False), (plus + 64 * count + here, True)]


def coefficient_row(k):
    return (k % TILES) * LANES + (k // TILES) * 64


def layer_kernel(
    table_ref,
    vectors_ref,
    source_ref,
    target_ref,
    live_ref,
    zero_hbm,
    one_hbm,
    two_hbm,
    out_ref,
    zero_ref,
    one_ref,
    two_ref,
    rot_ref,
    pick_ref,
    states_ref,
    rows_ref,
    left_ref,
    sum_ref,
    sems,
):
    loads = [
        pltpu.make_async_copy(src, dst, sems.at[index])
        for index, (src, dst) in enumerate(
            ((one_hbm, one_ref), (two_hbm, two_ref), (zero_hbm, zero_ref))
        )
    ]
    for load in loads:
        load.start()
    edges = source_ref.shape[1]
    vectors = jnp.concatenate([vectors_ref[part] for part in range(4)], axis=1)
    length = wigner_into(rot_ref, vectors)
    alive = lax.broadcasted_iota(jnp.int32, (1, edges), 1) < live_ref[0]
    scaling = jnp.where(alive, 0.5 * (jnp.cos(length * (math.pi / CUTOFF)) + 1.0), 0.0)
    source = jnp.broadcast_to(source_ref[...].astype(jnp.float32), (LANES, edges)).T
    lane = lax.broadcasted_iota(jnp.int32, (edges, LANES), 1).astype(jnp.float32)
    for part in range(8):
        pick_ref[:, part * LANES : (part + 1) * LANES] = jnp.where(
            source == lane + float(part * LANES), 1.0, 0.0
        ).astype(jnp.bfloat16)

    def pick_pair(first, count):
        right = [
            table_ref[:, first + step].reshape(1024, LANES) for step in range(count)
        ]
        right = right[0] if count == 1 else jnp.concatenate(right, axis=1)
        picked = jnp.dot(pick_ref[...], right, preferred_element_type=jnp.float32)
        rows = pl.ds(pl.multiple_of(first * LANES, LANES), count * LANES)
        states_ref[rows, :] = picked.astype(jnp.bfloat16).T

    def pick_step(step, carry):
        pick_pair(step * 2, 2)
        return carry

    lax.fori_loop(0, 12, pick_step, 0)
    pick_pair(24, 1)

    scale = jnp.broadcast_to(scaling, (16, edges))
    for degree in range(LMAX + 1):
        orders = min(2 * min(degree, MMAX) + 1, 5)
        base = degree * degree

        def turn(chunk, carry, degree=degree, orders=orders, base=base):
            start = pl.multiple_of(chunk * 16, 16)
            totals = [None] * orders
            for k in range(2 * degree + 1):
                rows = pl.ds(coefficient_row(base + k) + start, 16)
                value = states_ref[rows, :].astype(jnp.float32)
                for order in range(orders):
                    factor = rot_ref[base + k, order : order + 1, :]
                    term = factor * value
                    totals[order] = term if k == 0 else totals[order] + term
            for order in range(orders):
                result = totals[order] * scale
                for first, negate in left_rows(order, degree):
                    rows_ref[pl.ds(first + start, 16), :] = (
                        -result if negate else result
                    ).astype(jnp.bfloat16)
            return carry

        lax.fori_loop(0, 4, turn, 0)

    def flip(block, carry):
        rows = pl.ds(pl.multiple_of(block * LANES, LANES), LANES)
        left_ref[block] = rows_ref[rows, :].T
        return carry

    lax.fori_loop(0, LEFT_BLOCKS, flip, 0)
    sum_ref[...] = jnp.zeros_like(sum_ref)
    slot = lax.broadcasted_iota(jnp.int32, (16, edges), 0)
    chosen = jnp.where(slot == target_ref[...], 1.0, 0.0)

    def left(first, depth):
        blocks = [left_ref[first // LANES + i] for i in range(-(-depth // LANES))]
        whole = jnp.concatenate(blocks, axis=1)
        return whole[:, :depth]

    def mix(order, degree, start, depth, right):
        mixed = jnp.dot(left(start, depth), right, preferred_element_type=jnp.float32)
        mixed = mixed.astype(jnp.bfloat16)
        back = jnp.concatenate(
            [
                (rot_ref[degree * degree + k, order : order + 1, :] * chosen).astype(jnp.bfloat16)
                for k in range(2 * degree + 1)
            ],
            axis=0,
        )
        rows = pl.ds(16 * degree * degree, 16 * (2 * degree + 1))
        sum_ref[rows, :] += jnp.dot(back, mixed, preferred_element_type=jnp.float32)

    loads[0].wait()
    for degree in range(1, LMAX + 1):
        right = one_ref[:, :, degree - 1].reshape(768, 256)
        mix(1, degree, STARTS["p1"], 768, right)
        mix(2, degree, STARTS["n1"], 768, right)
    loads[1].wait()
    for degree in range(2, LMAX + 1):
        right = two_ref[:, :, degree - 2].reshape(640, 256)
        mix(3, degree, STARTS["p2"], 640, right)
        mix(4, degree, STARTS["n2"], 640, right)
    loads[2].wait()
    for degree in range(LMAX + 1):
        right = zero_ref[:, degree].reshape(448, 256)
        mix(0, degree, STARTS["z"], 448, right)
    for part in range(4):
        lanes = pl.ds(64 * part, 64)
        out_ref[part] = jnp.concatenate(
            [sum_ref[0:400, lanes], sum_ref[400:800, lanes]], axis=1
        ).astype(jnp.bfloat16)


def layer(table, vectors, source, target, live, zero, one, two):
    edges = source.shape[1]
    vmem = pl.BlockSpec(memory_space=pltpu.VMEM)
    hbm = pl.BlockSpec(memory_space=pl.ANY)
    return pl.pallas_call(
        layer_kernel,
        name="layer",
        out_shape=jax.ShapeDtypeStruct((4, 400, LANES), jnp.bfloat16),
        in_specs=[vmem, vmem, vmem, vmem, pl.BlockSpec(memory_space=pltpu.SMEM), hbm, hbm, hbm],
        out_specs=vmem,
        scratch_shapes=[
            pltpu.VMEM(zero.shape, jnp.bfloat16),
            pltpu.VMEM(one.shape, jnp.bfloat16),
            pltpu.VMEM(two.shape, jnp.bfloat16),
            pltpu.VMEM((COEFS, 8, edges), jnp.float32),
            pltpu.VMEM((edges, 1024), jnp.bfloat16),
            pltpu.VMEM((TILES * LANES, edges), jnp.bfloat16),
            pltpu.VMEM((LEFT_BLOCKS * LANES, edges), jnp.bfloat16),
            pltpu.VMEM((LEFT_BLOCKS, edges, LANES), jnp.bfloat16),
            pltpu.VMEM((800, 256), jnp.float32),
            pltpu.SemaphoreType.DMA((3,)),
        ],
        compiler_params=pltpu.CompilerParams(vmem_limit_bytes=60 << 20),
    )(table, vectors, source, target, live, zero, one, two)


def reduce_kernel(parts_ref, out_ref, landing, send, recv):
    edge = lax.axis_index("edge")
    chan = lax.axis_index("chan")
    barrier = pltpu.get_barrier_semaphore()
    for far in range(1, 4):
        pl.semaphore_signal(
            barrier,
            inc=1,
            device_id={"edge": edge, "chan": (chan + far) % 4},
            device_id_type=MESH,
        )
    pl.semaphore_wait(barrier, 3)
    copies = []
    for far in (2, 1, 3):
        target = (chan + far) % 4
        copy = pltpu.make_async_remote_copy(
            src_ref=parts_ref.at[target],
            dst_ref=landing.at[far - 1],
            send_sem=send.at[far - 1],
            recv_sem=recv.at[far - 1],
            device_id={"edge": edge, "chan": target},
            device_id_type=MESH,
        )
        copy.start()
        copies.append(copy)
    for copy in copies:
        copy.wait_recv()
    total = parts_ref[chan].astype(jnp.float32)
    for slot in range(3):
        total = total + landing[slot].astype(jnp.float32)
    out_ref[...] = total.astype(jnp.bfloat16)
    for copy in copies:
        copy.wait_send()


def reduce(parts):
    return pl.pallas_call(
        reduce_kernel,
        name="reduce_parts",
        out_shape=jax.ShapeDtypeStruct(parts.shape[1:], parts.dtype),
        in_specs=[pl.BlockSpec(memory_space=pltpu.VMEM)],
        out_specs=pl.BlockSpec(memory_space=pltpu.VMEM),
        scratch_shapes=[
            pltpu.VMEM((3, *parts.shape[1:]), parts.dtype),
            pltpu.SemaphoreType.DMA((3,)),
            pltpu.SemaphoreType.DMA((3,)),
        ],
        compiler_params=pltpu.CompilerParams(collective_id=1, has_side_effects=True),
    )(parts)


def shards(
    node_states,
    edge_vectors,
    source_part,
    source_slot,
    target_slot,
    live_edges,
    weight_zero,
    weight_one,
    weight_two,
):
    nodes = node_states.transpose(1, 0, 2)
    block = jnp.concatenate(
        [nodes[:TILES], jnp.pad(nodes[TILES:], ((0, 1), (0, 0), (0, 0)))], axis=2
    )
    vector = jnp.pad(edge_vectors, ((0, 5), (0, 0)))
    table, vectors = gather(block, vector)
    source = (source_part[:, 0] * node_states.shape[0] + source_slot)[None, :]
    parts = layer(
        table,
        vectors,
        source,
        target_slot[None, :],
        live_edges,
        weight_zero.transpose(0, 2, 1, 3),
        weight_one.transpose(0, 1, 3, 2, 4),
        weight_two.transpose(0, 1, 3, 2, 4),
    )
    total = reduce(parts).reshape(TILES, 16, LANES)
    result = jnp.concatenate([total[:, :, :64], total[: COEFS - TILES, :, 64:]], axis=0)
    return result.transpose(1, 0, 2)


def solution(mesh):
    in_specs = (
        P("edge", None, "chan"),
        P(None, ("edge", "chan")),
        P("edge", None),
        P("edge"),
        P("edge"),
        P("edge"),
        P(None, "chan", None, None),
        P(None, None, "chan", None, None),
        P(None, None, "chan", None, None),
    )
    out_specs = P("edge", None, "chan")
    return jax.shard_map(shards, mesh=mesh, in_specs=in_specs, out_specs=out_specs, check_vma=False)
```

time: 410 us -> 101 us (0.25)
  waiting for transfers between devices: 247 us -> 0 us
  Pallas kernels: 0 us -> 90 us
  local copies, waits for them, and re-layouts: 75.8 us -> 6.8 us
  matrix products: 30.5 us -> 0 us
  other arithmetic: 26.9 us -> 3.66 us
  between operations: 18.1 us -> 0.7 us
  blocking collectives: 10.5 us -> 0 us
    all_gather x1 -> x0, waiting for transfers between devices: 173 us -> none  [shards(): table = lax.all_gather(node_flat, 'edge', axis=0, tiled=True)]
    pallas_call x0 -> x3, Pallas kernels: none -> 90 us  [the longest x1 50 us: gather(): pl.pallas_call(gather_kernel, name='gather_table', out_shape=(jax.ShapeDt...]
    unnamed x3 -> x0, waiting for transfers between devices: 73.7 us -> none
    unnamed x534 -> x4, local copies, waits for them, and re-layouts: 36.1 us -> 3.33 us
    dot_general x43 -> x0, matrix products: 30.5 us -> none  [the longest x1 8.62 us: shards(): lax.dot_general(table, select, (((0,), (1,)), ((), ())), preferred_elemen...]
    mul x28 -> x0, local copies, waits for them, and re-layouts: 30.4 us -> none  [shards(): compact_t[offset:offset + span][None] * selector[:, None]]
    mul x22 -> x1, other arithmetic: 14.9 us -> 0.69 us  [shards(): source = (source_part[:, 0] * node_states.shape[0] + source_slot)[None, :]]
    all_gather x1 -> x0, blocking collectives: 10.5 us -> none  [shards(): packed_t = lax.all_gather(packed, 'chan', axis=0, tiled=True).T]
  transfers between devices with their start and end apart: 2 -> 0, of which waited for: 2 -> 0; matrix products, arithmetic and copies ran while one was open for 20% -> 0% of each run, Pallas kernels for 0% -> 0%
where the time goes in v2:
time: 101 us
  Pallas kernels  90 us (89%)
  local copies, waits for them, and re-layouts  6.8 us (7%)
  other arithmetic  3.66 us (4%)
    pallas_call x1, Pallas kernels, gather(): pl.pallas_call(gather_kernel, name='gather_table', out_shape=(jax.ShapeDt...  50 us
    pallas_call x1, Pallas kernels, layer(): pl.pallas_call(layer_kernel, name='layer', out_shape=jax.ShapeDtypeStruct...  27.5 us
    pallas_call x1, Pallas kernels, reduce(): pl.pallas_call(reduce_kernel, name='reduce_parts', out_shape=jax.ShapeDty...  12.5 us
    unnamed x4, local copies, waits for them, and re-layouts  3.33 us

profile of v2, /device:TPU:1, one launch (start us, length us, event | category | flops | bytes accessed | tf_op | source)
XLA Modules:
  0.0 101.2 jit_solution(2149659841145508279)
XLA Ops:
  0.7 0.7 broadcast_multiply_fusion
  1.3 1.3 %add.7 = s32[512]{0:T(512)} add(s32[512]{0:T(512)S(1)} %bitcast.19, s32[512]{0:T(512)} %param.12) | non-fusion elementwise | flops 512 | bytes 6144 | tf_op jit(solution)/shard_map/add | solution.py:570
  2.6 0.7 pad.9.vector_ref
  3.3 0.9 slice.17
  4.2 0.9 slice.16
  5.1 0.1 fusion.1.block_ref
  5.2 50.0 %gather_table.1 = (bf16[64,25,16,128]{3,2,1,0:T(8,128)(2,1)S(1)}, f32[4,8,128]{2,1,0:T(8,128)S(1)}) custom-call(bf16[25,16,128]{2,1,0:T(8,128)(2,1)S(1)} %fusion.1.block_ref, f32[8,128]{1,0:T(8,128)S(1)} %pad.9.vector_ref), custom_call_target="tpu_custom_call" | custom-call | tf_op jit(solution)/shard_map/gather_table/pallas_call | solution.py:303
  55.2 0.0 copy-start
  55.3 2.7 %copy-done = bf16[64,25,16,128]{3,2,1,0:T(8,128)(2,1)} copy-done((bf16[64,25,16,128]{3,2,1,0:T(8,128)(2,1)}, bf16[64,25,16,128]{3,2,1,0:T(8,128)(2,1)S(1)}, u32[]{:S(2)}) %copy-start) | copy-done | bytes 6553624
  58.0 0.0 copy-start.1
  58.0 0.6 copy-done.1
  58.6 27.5 %layer.1.parts_ref = bf16[4,400,128]{2,1,0:T(8,128)(2,1)} custom-call(bf16[64,25,16,128]{3,2,1,0:T(8,128)(2,1)} %copy-done, f32[4,8,128]{2,1,0:T(8,128)} %copy-done.1, s32[1,512]{1,0:T(1,128)} %bitcast.18, s32[1,512]{1,0:T(1,128)} %bitcast.20, s32[1]{0:T(128)S(6)} %copy.10.live_ref, bf16[7,7,64,256]{3,2,1,0:T(8,128)(2,1)} %bitcast.13, ...), custom_call_target="tpu_custom_call" | custom-call | tf_op jit(solution)/shard_map/layer/pallas_call | solution.py:480
  86.1 12.5 %reduce_parts.1 = bf16[400,128]{1,0:T(8,128)(2,1)} custom-call(bf16[4,400,128]{2,1,0:T(8,128)(2,1)} %layer.1.parts_ref), custom_call_target="tpu_custom_call" | custom-call | tf_op jit(solution)/shard_map/reduce_parts/pallas_call | solution.py:538
  98.6 1.0 slice.19
  99.6 1.6 %maximum_bitcast_fusion = bf16[16,49,64]{2,0,1:T(8,128)(2,1)} fusion(bf16[24,16,64]{2,1,0:T(8,128)(2,1)S(1)} %slice.19, bf16[25,16,64]{2,1,0:T(8,128)(2,1)} %bitcast.15), kind=kLoop, calls=%fused_computation.2 | loop fusion | flops 50176 | bytes 200704 | tf_op jit(solution)/shard_map/transpose | solution.py:583
Async XLA Ops:
  55.2 2.7 %copy-start = (bf16[64,25,16,128]{3,2,1,0:T(8,128)(2,1)}, bf16[64,25,16,128]{3,2,1,0:T(8,128)(2,1)S(1)}, u32[]{:S(2)}) copy-start(bf16[64,25,16,128]{3,2,1,0:T(8,128)(2,1)S(1)} %get-tuple-element.7.table_ref) | copy-start | bytes 19660804
  58.0 0.6 copy-start.1

commit v3 on v2

v3 whole, which is shorter than its diff:
```python
import math

import jax
import jax.numpy as jnp
import numpy as np
from jax import lax
from jax.experimental import pallas as pl
from jax.experimental.pallas import tpu as pltpu
from jax.sharding import PartitionSpec as P

LMAX = 6
MMAX = 2
COEFS = (LMAX + 1) ** 2
CUTOFF = 6.0
LANES = 128
TILES = 25
MESH = pl.DeviceIdType.MESH

Y_RING, Z_RING = 4, 8
STEP = {"y+": (1, 0), "y-": (-1, 0), "z+": (0, 1), "z-": (0, -1), "x": (0, 0)}
COLOURS = {
    "py": ("y", True, ((0, 3), (3, 6))),
    "sy": ("y", False, ((6, 8), (8, 10))),
    "pz": ("z", True, ((10, 15), (15, 19))),
    "sz": ("z", False, ((19, 22), (22, 25))),
}
Y_TILES = 10
LATENCY, BYTES_PER_US, BLOCK_TILE = 1.8, 46.6e3, 4096


def schedule():
    free = {link: 0.0 for link in STEP}
    waiting = {link: [] for link in STEP}
    events, sends, begun, landed = [], [], [], []
    count = 0

    def put(link, time, rank, colour, half, oy, oz):
        nonlocal count
        waiting[link].append((time, -rank, count, colour, half, oy, oz))
        count += 1

    def follow(time, colour, half, oy, oz, via):
        axis_first, paired, _ = COLOURS[colour]
        if via == "x" and not paired:
            return
        via = "" if via == "x" else via
        if not paired:
            put("x", time, 0, colour, half, oy, oz)
        second = "z" if axis_first == "y" else "y"
        offset = {"y": oy, "z": oz}
        limit = {"y": Y_RING // 2, "z": Z_RING // 2}

        def along(axis, rank):
            moved = offset[axis]
            for sign, mine in (("+", 0), ("-", 1)):
                hops = abs(moved) + 1
                if (moved != 0 and via != axis + sign) or hops > limit[axis]:
                    continue
                taken = (mine,) if hops == limit[axis] else half
                taken = tuple(h for h in taken if h in half)
                if taken:
                    put(axis + sign, time, rank + limit[axis] - hops, colour, taken, oy, oz)

        if offset[second] == 0:
            along(axis_first, 10)
        along(second, 0)

    for colour, (_, paired, _) in COLOURS.items():
        if paired:
            put("x", 0.0, 20, colour, (0, 1), 0, 0)
        else:
            follow(0.0, colour, (0, 1), 0, 0, "")
    while events or any(waiting.values()):
        ready = [
            (max(free[link], min(item[0] for item in items)), link)
            for link, items in waiting.items()
            if items
        ]
        begin = min(ready) if ready else None
        if events and (begin is None or min(events)[0] <= begin[0]):
            event = min(events)
            events.remove(event)
            time, _, colour, half, oy, oz, via = event
            follow(time, colour, half, oy, oz, via)
            continue
        time, link = begin
        item = min(
            (item for item in waiting[link] if item[0] <= time),
            key=lambda it: (it[1], it[0], it[2]),
        )
        waiting[link].remove(item)
        known, _, _, colour, half, oy, oz = item
        _, paired, halves = COLOURS[colour]
        first, end = halves[half[0]][0], halves[half[-1]][1]
        both = paired and link != "x"
        free[link] = time + (end - first) * (2 if both else 1) * BLOCK_TILE / BYTES_PER_US
        earlier = [b for b, s in zip(begun, sends) if s[0] == link]
        dy, dz = STEP[link]
        sends.append((link, both, first, end, oy, oz))
        begun.append(max([known] + earlier[-1:]))
        landed.append(free[link] + LATENCY)
        events.append((landed[-1], count, colour, half, oy - dy, oz - dz, link))
        count += 1
    steps = [(time, 1, index, "send") for index, time in enumerate(begun)]
    steps += [(time, 0, index, "wait") for index, time in enumerate(landed)]
    return sends, [(kind, index) for _, _, index, kind in sorted(steps)]


SENDS, PROGRAM = schedule()


def brought(index):
    link, both, first, end, oy, oz = SENDS[index]
    dy, dz = STEP[link]
    sides = ("own", "other") if both else (("other",) if link == "x" else ("own",))
    return {
        (tile, (oy - dy) % Y_RING, (oz - dz) % Z_RING, side)
        for tile in range(first, end)
        for side in sides
    }


def harmonics_at(points, degree_top):
    x, y, z = points
    rows = {}
    real, imag = [np.ones_like(x)], [np.zeros_like(x)]
    for m in range(1, degree_top + 1):
        real.append(x * real[m - 1] - y * imag[m - 1])
        imag.append(x * imag[m - 1] + y * real[m - 1])
    for m in range(degree_top + 1):
        start = (-1.0) ** m * math.prod(range(2 * m - 1, 0, -2))
        legendre = {m: np.full_like(z, start), m + 1: z * ((2 * m + 1) * start)}
        for l in range(m + 2, degree_top + 1):
            legendre[l] = (
                (2 * l - 1) * z * legendre[l - 1] - (l + m - 1) * legendre[l - 2]
            ) / (l - m)
        for l in range(m, degree_top + 1):
            factor = math.sqrt(
                (2 * l + 1) / (4 * math.pi) * math.factorial(l - m) / math.factorial(l + m)
            )
            if m == 0:
                rows[l, 0] = factor * legendre[l]
            else:
                rows[l, m] = math.sqrt(2.0) * factor * legendre[l] * real[m]
                rows[l, -m] = math.sqrt(2.0) * factor * legendre[l] * imag[m]
    return np.stack([rows[l, m] for l in range(degree_top + 1) for m in range(-l, l + 1)])


def raising_tables():
    count = 4 * (LMAX + 2) ** 2
    at = np.arange(count) + 0.5
    height = 1.0 - 2.0 * at / count
    radius = np.sqrt(1.0 - height * height)
    angle = math.pi * (3.0 - math.sqrt(5.0)) * at
    points = np.stack([radius * np.cos(angle), radius * np.sin(angle), height])
    basis = harmonics_at(points, LMAX)
    inverse = np.linalg.pinv(basis.T)
    tables = {}
    for l in range(1, LMAX + 1):
        below = basis[(l - 1) ** 2 : l * l]
        tables[l] = [
            np.where(np.abs(part) < 1e-9, 0.0, part)
            for part in (
                (inverse @ (points[c] * below).T)[l * l : (l + 1) ** 2] for c in range(3)
            )
        ]
    return tables


RAISE = raising_tables()


def project(table, degree, weights, rows):
    results = []
    for m in range(2 * degree + 1):
        total = None
        for axis in range(3):
            for n in range(2 * degree - 1):
                value = float(table[axis][m, n])
                if value != 0.0:
                    term = (value * weights[axis]) * rows[n]
                    total = term if total is None else total + term
        results.append(total)
    return results


def wigner_into(rot_ref, vectors):
    x, y, z = vectors[0:1], vectors[1:2], vectors[2:3]
    length = jnp.sqrt(x * x + y * y + z * z)
    u = [x / length, y / length, z / length]
    pick = jnp.where(jnp.abs(u[0]) < 0.6, 1.0, 0.0)
    other = 1.0 - pick
    a = [-u[2] * other, u[2] * pick, u[0] * other - u[1] * pick]
    norm = jnp.sqrt(a[0] * a[0] + a[1] * a[1] + a[2] * a[2])
    a = [part / norm for part in a]
    b = [
        u[1] * a[2] - u[2] * a[1],
        u[2] * a[0] - u[0] * a[2],
        u[0] * a[1] - u[1] * a[0],
    ]
    shape = (8, x.shape[1])
    order = lax.broadcasted_iota(jnp.int32, shape, 0)
    wide = [jnp.broadcast_to(part, shape) for part in u]
    below = [jnp.where(order == 0, 1.0, 0.0)]
    rot_ref[0] = below[0]
    for l in range(1, LMAX + 1):
        table = RAISE[l]
        inverse = [1.0 / float(table[2][m + l, m + l - 1]) if m < l else 0.0 for m in range(3)]
        scale = jnp.where(
            order == 0, inverse[0], jnp.where(order <= 2, inverse[1], inverse[2])
        )
        rows = project(table, l, [part * scale for part in wide], below)
        rows = [jnp.zeros(shape, jnp.float32) if row is None else row for row in rows]
        if l == 1:
            first = project(table, 1, a, [1.0])
            second = project(table, 1, b, [1.0])
            one = 1.0 / float(table[0][2, 0])
            two = 1.0 / float(table[1][0, 0])
            rows = [
                jnp.where(order == 1, one * f, jnp.where(order == 2, two * s, r))
                for f, s, r in zip(first, second, rows)
            ]
        if l == 2:
            plus = [row[1:2] for row in below]
            minus = [row[2:3] for row in below]
            aa, bb = project(table, 2, a, plus), project(table, 2, b, minus)
            ab, ba = project(table, 2, a, minus), project(table, 2, b, plus)
            one = 1.0 / float(table[0][4, 2] - table[1][4, 0])
            two = 1.0 / float(table[0][0, 0] + table[1][0, 2])
            rows = [
                jnp.where(
                    order == 3,
                    one * (aa[m] - bb[m]),
                    jnp.where(order == 4, two * (ab[m] + ba[m]), rows[m]),
                )
                for m in range(5)
            ]
        for k, row in enumerate(rows):
            rot_ref[l * l + k] = row
        below = rows
    return length


STARTS = {"p1": 0, "n1": 768, "p2": 1536, "n2": 2176, "z": 2816}
LEFT_BLOCKS = 26


def left_rows(order, degree):
    if order == 0:
        return [(STARTS["z"] + 64 * degree, False)]
    m = (order + 1) // 2
    count = LMAX + 1 - m
    plus, minus = STARTS["p%d" % m], STARTS["n%d" % m]
    here = 64 * (degree - m)
    if order % 2:
        return [(plus + here, False), (minus + 64 * count + here, False)]
    return [(minus + here, False), (plus + 64 * count + here, True)]


def coefficient_row(k):
    return (k % TILES) * LANES + (k // TILES) * 64


GROUPS = [("z", (0, 1, 7)), ("y", (0,)), ("z", (2, 6)), ("y", (1, 3)), ("z", (3, 5, 4)), ("y", (2,))]


def group_tiles(axis):
    return range(0, Y_TILES) if axis == "z" else range(Y_TILES, TILES)


def group_needs(axis, offsets):
    return {
        (tile, oy, oz, side)
        for tile in group_tiles(axis)
        for oy in (range(Y_RING) if axis == "z" else offsets)
        for oz in (offsets if axis == "z" else range(Z_RING))
        for side in ("own", "other")
    }


PIECES = [((6, 5), 25, 12, 12), ((4, 3), 9, 8, 8), ((2, 1, 0), 0, 5, 4)]


def layer_kernel(
    nodes_ref,
    vector_ref,
    part_ref,
    slot_ref,
    target_ref,
    live_ref,
    zero_hbm,
    one_hbm,
    two_hbm,
    out_ref,
    table_ref,
    vectors_ref,
    zero_ref,
    one_ref,
    two_ref,
    rot_ref,
    pick_ref,
    states_ref,
    rows_ref,
    left_ref,
    sum_ref,
    parts_ref,
    landing_ref,
    send,
    recv,
    local,
    spread_sems,
    part_sems,
):
    edge = lax.axis_index("edge")
    chan = lax.axis_index("chan")
    edges = part_ref.shape[1]
    x = edge % 2
    z = (edge // 2) % Z_RING
    y = edge // (2 * Z_RING)

    def wrap(position, offset, size):
        return (position + (offset % size)) % size

    def device(dy, dz, side):
        return (wrap(y, dy, Y_RING) * Z_RING + wrap(z, dz, Z_RING)) * 2 + side

    reach = {link: device(dy, dz, x) for link, (dy, dz) in STEP.items() if link != "x"}
    reach["x"] = device(0, 0, 1 - x)
    barrier = pltpu.get_barrier_semaphore()
    for target in reach.values():
        pl.semaphore_signal(
            barrier, inc=1, device_id={"edge": target, "chan": chan}, device_id_type=MESH
        )
    for far in range(1, 4):
        pl.semaphore_signal(
            barrier,
            inc=1,
            device_id={"edge": edge, "chan": (chan + far) % 4},
            device_id_type=MESH,
        )
    loads = [
        pltpu.make_async_copy(src, dst, local.at[index])
        for index, (src, dst) in enumerate(
            ((one_hbm, one_ref), (two_hbm, two_ref), (zero_hbm, zero_ref))
        )
    ]
    for tile in range(TILES):
        low = nodes_ref[tile]
        high = nodes_ref[tile + TILES] if tile + TILES < COEFS else jnp.zeros_like(low)
        table_ref[y, z, x, tile] = jnp.concatenate([low, high], axis=1)
    vectors_ref[chan] = vector_ref[...]
    pl.semaphore_wait(barrier, 8)

    copies = []
    for index, (link, both, first, end, oy, oz) in enumerate(SENDS):
        view = table_ref.at[
            wrap(y, oy, Y_RING),
            wrap(z, oz, Z_RING),
            pl.ds(0, 2) if both else pl.ds(x, 1),
            pl.ds(first, end - first),
        ]
        copies.append(
            pltpu.make_async_remote_copy(
                src_ref=view,
                dst_ref=view,
                send_sem=send.at[index],
                recv_sem=recv.at[index],
                device_id={"edge": reach[link], "chan": chan},
                device_id_type=MESH,
            )
        )
    spread = [
        pltpu.make_async_remote_copy(
            src_ref=vector_ref,
            dst_ref=vectors_ref.at[chan],
            send_sem=spread_sems.at[far - 1],
            recv_sem=spread_sems.at[far + 2],
            device_id={"edge": edge, "chan": (chan + far) % 4},
            device_id_type=MESH,
        )
        for far in range(1, 4)
    ]

    scaling = []

    def begin_loads():
        for load in loads:
            load.start()

    def make_rotation():
        for copy in spread:
            copy.wait_recv()
        vectors = jnp.concatenate([vectors_ref[part] for part in range(4)], axis=1)
        length = wigner_into(rot_ref, vectors)
        alive = lax.broadcasted_iota(jnp.int32, (1, edges), 1) < live_ref[0]
        scaling.append(
            jnp.where(alive, 0.5 * (jnp.cos(length * (math.pi / CUTOFF)) + 1.0), 0.0)
        )

    def make_pick():
        source = part_ref[...] * 16 + slot_ref[...]
        row = lax.broadcasted_iota(jnp.int32, (32, edges), 0)
        for part in range(Y_RING * Z_RING):
            pick_ref[part // Z_RING, part % Z_RING] = jnp.where(
                source == row + 32 * part, 1.0, 0.0
            ).astype(jnp.bfloat16)

    def pick(axis, offsets, first, count, fresh):
        right, left = [], []
        for offset in offsets:
            if axis == "z":
                where = wrap(z, offset, Z_RING)
                right.append(pick_ref[:, where].reshape(128, edges))
            else:
                where = wrap(y, offset, Y_RING)
                right.append(pick_ref[where].reshape(256, edges))
            tiles = []
            for tile in range(first, first + count):
                if axis == "z":
                    part = table_ref[:, where, :, tile].reshape(128, LANES)
                else:
                    part = table_ref[where, :, :, tile].reshape(256, LANES)
                tiles.append(part.T)
            left.append(jnp.concatenate(tiles, axis=0) if count > 1 else tiles[0])
        left = jnp.concatenate(left, axis=1) if len(left) > 1 else left[0]
        right = jnp.concatenate(right, axis=0) if len(right) > 1 else right[0]
        picked = jnp.dot(left, right, preferred_element_type=jnp.float32).astype(jnp.bfloat16)
        rows = pl.ds(first * LANES, count * LANES)
        states_ref[rows, :] = picked if fresh else states_ref[rows, :] + picked

    have = {(tile, 0, 0, "own") for tile in range(TILES)}
    groups = list(GROUPS)
    seen = set()
    work = [begin_loads, make_pick, make_rotation]
    for kind, index in PROGRAM:
        if kind == "send":
            copies[index].start()
            if index == 3:
                for copy in spread:
                    copy.start()
            continue
        if index >= 10 and work:
            work.pop(0)()
        copies[index].wait_recv()
        have |= brought(index)
        while groups and group_needs(*groups[0]) <= have:
            axis, offsets = groups.pop(0)
            tiles = group_tiles(axis)
            for first in range(tiles[0], tiles[-1] + 1, 2):
                count = min(2, tiles[-1] + 1 - first)
                fresh = axis not in seen
                work.append(
                    lambda a=axis, o=offsets, f=first, c=count, n=fresh: pick(a, o, f, c, n)
                )
            seen.add(axis)
    for item in work:
        item()

    scale = jnp.broadcast_to(scaling[0], (16, edges))
    for degree in range(LMAX + 1):
        orders = 2 * min(degree, MMAX) + 1
        base = degree * degree

        def turn(chunk, carry, degree=degree, orders=orders, base=base):
            start = pl.multiple_of(chunk * 16, 16)
            totals = [None] * orders
            for k in range(2 * degree + 1):
                rows = pl.ds(coefficient_row(base + k) + start, 16)
                value = states_ref[rows, :].astype(jnp.float32)
                for order in range(orders):
                    factor = rot_ref[base + k, order : order + 1, :]
                    term = factor * value
                    totals[order] = term if k == 0 else totals[order] + term
            for order in range(orders):
                result = totals[order] * scale
                for first, negate in left_rows(order, degree):
                    rows_ref[pl.ds(first + start, 16), :] = (
                        -result if negate else result
                    ).astype(jnp.bfloat16)
            return carry

        lax.fori_loop(0, 4, turn, 0)

    def flip(block, carry):
        rows = pl.ds(pl.multiple_of(block * LANES, LANES), LANES)
        left_ref[block] = rows_ref[rows, :].T
        return carry

    lax.fori_loop(0, LEFT_BLOCKS, flip, 0)
    slot = lax.broadcasted_iota(jnp.int32, (16, edges), 0)
    chosen = jnp.where(slot == target_ref[...], 1.0, 0.0)

    def left(first, depth):
        blocks = [left_ref[first // LANES + i] for i in range(-(-depth // LANES))]
        return jnp.concatenate(blocks, axis=1)[:, :depth]

    def mix(order, degree, start, depth, right):
        mixed = jnp.dot(left(start, depth), right, preferred_element_type=jnp.float32)
        mixed = mixed.astype(jnp.bfloat16)
        back = jnp.concatenate(
            [
                (rot_ref[degree * degree + k, order : order + 1, :] * chosen).astype(jnp.bfloat16)
                for k in range(2 * degree + 1)
            ],
            axis=0,
        )
        rows = pl.ds(16 * degree * degree, 16 * (2 * degree + 1))
        value = jnp.dot(back, mixed, preferred_element_type=jnp.float32)
        sum_ref[rows, :] = value if order == 0 else sum_ref[rows, :] + value

    for load in loads:
        load.wait()
    outgoing = []
    base = 0
    for number, (degrees, first, lows, highs) in enumerate(PIECES):
        for degree in degrees:
            mix(0, degree, STARTS["z"], 448, zero_ref[:, degree].reshape(448, 256))
            if degree >= 1:
                right = one_ref[:, :, degree - 1].reshape(768, 256)
                mix(1, degree, STARTS["p1"], 768, right)
                mix(2, degree, STARTS["n1"], 768, right)
            if degree >= 2:
                right = two_ref[:, :, degree - 2].reshape(640, 256)
                mix(3, degree, STARTS["p2"], 640, right)
                mix(4, degree, STARTS["n2"], 640, right)
        for part in range(4):
            lanes = pl.ds(64 * part, 64)
            low = sum_ref[pl.ds(16 * first, 16 * lows), lanes]
            high = sum_ref[pl.ds(16 * (first + lows), 16 * highs), lanes]
            if highs < lows:
                high = jnp.concatenate(
                    [high, jnp.zeros((16 * (lows - highs), 64), jnp.float32)], axis=0
                )
            parts_ref[part, pl.ds(16 * base, 16 * lows)] = jnp.concatenate(
                [low, high], axis=1
            ).astype(jnp.bfloat16)
        piece = []
        for far in (2, 1, 3):
            target = (chan + far) % 4
            copy = pltpu.make_async_remote_copy(
                src_ref=parts_ref.at[target, pl.ds(16 * base, 16 * lows)],
                dst_ref=landing_ref.at[far - 1, pl.ds(16 * base, 16 * lows)],
                send_sem=part_sems.at[0, number, far - 1],
                recv_sem=part_sems.at[1, number, far - 1],
                device_id={"edge": edge, "chan": target},
                device_id_type=MESH,
            )
            copy.start()
            piece.append(copy)
        outgoing.append((base, piece))
        base += lows
    for (base, piece), (degrees, first, lows, highs) in zip(outgoing, PIECES):
        for copy in piece:
            copy.wait_recv()
        rows = pl.ds(16 * base, 16 * lows)
        total = parts_ref[chan, rows].astype(jnp.float32)
        for slot_number in range(3):
            total = total + landing_ref[slot_number, rows].astype(jnp.float32)
        total = total.astype(jnp.bfloat16)
        for step in range(lows):
            out_ref[first + step] = total[16 * step : 16 * step + 16, :64]
        for step in range(highs):
            out_ref[first + lows + step] = total[16 * step : 16 * step + 16, 64:]
    for copy in copies + spread:
        copy.wait_send()
    for _, piece in outgoing:
        for copy in piece:
            copy.wait_send()


def shards(
    node_states,
    edge_vectors,
    source_part,
    source_slot,
    target_slot,
    live_edges,
    weight_zero,
    weight_one,
    weight_two,
):
    edges = source_slot.shape[0]
    zero = weight_zero.transpose(0, 2, 1, 3)
    one = weight_one.transpose(0, 1, 3, 2, 4)
    two = weight_two.transpose(0, 1, 3, 2, 4)
    vmem = pl.BlockSpec(memory_space=pltpu.VMEM)
    hbm = pl.BlockSpec(memory_space=pl.ANY)
    result = pl.pallas_call(
        layer_kernel,
        name="layer",
        out_shape=jax.ShapeDtypeStruct((COEFS, 16, 64), jnp.bfloat16),
        in_specs=[vmem] * 5 + [pl.BlockSpec(memory_space=pltpu.SMEM), hbm, hbm, hbm],
        out_specs=vmem,
        scratch_shapes=[
            pltpu.VMEM((Y_RING, Z_RING, 2, TILES, 16, LANES), jnp.bfloat16),
            pltpu.VMEM((4, 3, LANES), jnp.float32),
            pltpu.VMEM(zero.shape, jnp.bfloat16),
            pltpu.VMEM(one.shape, jnp.bfloat16),
            pltpu.VMEM(two.shape, jnp.bfloat16),
            pltpu.VMEM((COEFS, 8, edges), jnp.float32),
            pltpu.VMEM((Y_RING, Z_RING, 32, edges), jnp.bfloat16),
            pltpu.VMEM((TILES * LANES, edges), jnp.bfloat16),
            pltpu.VMEM((LEFT_BLOCKS * LANES, edges), jnp.bfloat16),
            pltpu.VMEM((LEFT_BLOCKS, edges, LANES), jnp.bfloat16),
            pltpu.VMEM((16 * COEFS, 256), jnp.float32),
            pltpu.VMEM((4, 400, LANES), jnp.bfloat16),
            pltpu.VMEM((3, 400, LANES), jnp.bfloat16),
            pltpu.SemaphoreType.DMA((len(SENDS),)),
            pltpu.SemaphoreType.DMA((len(SENDS),)),
            pltpu.SemaphoreType.DMA((3,)),
            pltpu.SemaphoreType.DMA((6,)),
            pltpu.SemaphoreType.DMA((2, 3, 3)),
        ],
        compiler_params=pltpu.CompilerParams(
            collective_id=0, has_side_effects=True, vmem_limit_bytes=60 << 20
        ),
    )(
        node_states.transpose(1, 0, 2),
        edge_vectors,
        source_part.reshape(1, edges),
        source_slot.reshape(1, edges),
        target_slot.reshape(1, edges),
        live_edges,
        zero,
        one,
        two,
    )
    return result.transpose(1, 0, 2)


def solution(mesh):
    in_specs = (
        P("edge", None, "chan"),
        P(None, ("edge", "chan")),
        P("edge", None),
        P("edge"),
        P("edge"),
        P("edge"),
        P(None, "chan", None, None),
        P(None, None, "chan", None, None),
        P(None, None, "chan", None, None),
    )
    out_specs = P("edge", None, "chan")
    return jax.shard_map(shards, mesh=mesh, in_specs=in_specs, out_specs=out_specs, check_vma=False)
```

time: 101 us -> 76.8 us (0.76)
  Pallas kernels: 90 us -> 74.4 us
  local copies, waits for them, and re-layouts: 6.8 us -> 1.62 us
  other arithmetic: 3.66 us -> 0 us
    pallas_call x3 -> x1, Pallas kernels: 90 us -> 74.4 us  [shards(): pl.pallas_call(layer_kernel, name='layer', out_shape=jax.ShapeDtypeStruct...]
    slice x3 -> x0, local copies, waits for them, and re-layouts: 2.78 us -> none  [the longest x1 0.98 us: shards(): total[:COEFS - TILES, :, 64:]]
    unnamed x4 -> x1, local copies, waits for them, and re-layouts: 3.33 us -> 1.62 us
    transpose x1 -> x0, other arithmetic: 1.62 us -> none  [shards(): return result.transpose(1, 0, 2)]
    add x1 -> x0, other arithmetic: 1.26 us -> none  [shards(): source = (source_part[:, 0] * node_states.shape[0] + source_slot)[None, :]]
where the time goes in v3:
time: 76.8 us; the launch traced here: 76.7 us
  Pallas kernels  74.4 us (97%)
  local copies, waits for them, and re-layouts  1.62 us (2%)
    pallas_call x1, Pallas kernels, shards(): pl.pallas_call(layer_kernel, name='layer', out_shape=jax.ShapeDtypeStruct...  74.4 us
    unnamed x1, local copies, waits for them, and re-layouts  1.62 us

profile of v3, /device:TPU:1, one launch (start us, length us, event | category | flops | bytes accessed | tf_op | source)
XLA Modules:
  0.0 76.7 jit_solution(11764893574859149263)
XLA Ops:
  0.7 74.4 %layer.1 = bf16[49,16,64]{2,1,0:T(8,128)(2,1)} custom-call(bf16[49,16,64]{2,1,0:T(8,128)(2,1)} %bitcast.12, f32[3,128]{1,0:T(4,128)} %vector_ref.1, s32[1,512]{1,0:T(1,128)} %bitcast.13, s32[1,512]{1,0:T(1,128)} %bitcast.14, s32[1,512]{1,0:T(1,128)} %bitcast.15, s32[1]{0:T(128)S(6)} %copy.11.live_ref, bf16[7,7,64,256]{3,2,1,0:T(8,128)(2,1)} %bitcast.10, ...), custom_call_target="tpu_custom_call" | custom-call | tf_op jit(solution)/shard_map/layer/pallas_call | solution.py:588
  75.1 1.6 %copy.12 = bf16[16,49,64]{2,0,1:T(8,128)(2,1)} copy(bf16[16,49,64]{2,0,1:T(8,128)(2,1)} %bitcast.11) | data formatting | bytes 200704

commit v4 on v3

--- a/solution.py
+++ b/solution.py
@@ -25,27 +25,32 @@
     "sz": ("z", False, ((19, 22), (22, 25))),
 }
 Y_TILES = 10
-LATENCY, BYTES_PER_US, BLOCK_TILE = 1.8, 46.6e3, 4096
+LATENCY, BYTES_PER_US, BLOCK_TILE, SLACK = 2.8, 46e3, 4096, 3.0
 
 
 def schedule():
     free = {link: 0.0 for link in STEP}
     waiting = {link: [] for link in STEP}
-    events, sends, begun, landed = [], [], [], []
+    events, sends, begun, landed, passed = [], [], [], [], set()
     count = 0
 
-    def put(link, time, rank, colour, half, oy, oz):
+    def put(link, time, rank, colour, half, oy, oz, sides):
         nonlocal count
-        waiting[link].append((time, -rank, count, colour, half, oy, oz))
+        waiting[link].append((time, -rank, count, colour, half, oy, oz, sides))
         count += 1
 
-    def follow(time, colour, half, oy, oz, via):
+    def follow(time, colour, half, oy, oz, via, brings):
         axis_first, paired, _ = COLOURS[colour]
+        sides = "both" if paired else "own"
         if via == "x" and not paired:
             return
-        via = "" if via == "x" else via
+        if via not in ("", "x") and paired and brings == "own":
+            return
+        if not via or via == "x":
+            sides = "own" if not via else "other"
+            via = ""
         if not paired:
-            put("x", time, 0, colour, half, oy, oz)
+            put("x", time, 0, colour, half, oy, oz, "own")
         second = "z" if axis_first == "y" else "y"
         offset = {"y": oy, "z": oz}
         limit = {"y": Y_RING // 2, "z": Z_RING // 2}
@@ -59,7 +64,16 @@
                 taken = (mine,) if hops == limit[axis] else half
                 taken = tuple(h for h in taken if h in half)
                 if taken:
-                    put(axis + sign, time, rank + limit[axis] - hops, colour, taken, oy, oz)
+                    put(
+                        axis + sign,
+                        time,
+                        rank + limit[axis] - hops + (0 if paired else 1),
+                        colour,
+                        taken,
+                        oy,
+                        oz,
+                        sides,
+                    )
 
         if offset[second] == 0:
             along(axis_first, 10)
@@ -67,9 +81,8 @@
 
     for colour, (_, paired, _) in COLOURS.items():
         if paired:
-            put("x", 0.0, 20, colour, (0, 1), 0, 0)
-        else:
-            follow(0.0, colour, (0, 1), 0, 0, "")
+            put("x", 0.0, 20, colour, (0, 1), 0, 0, "own")
+        follow(0.0, colour, (0, 1), 0, 0, "", "own")
     while events or any(waiting.values()):
         ready = [
             (max(free[link], min(item[0] for item in items)), link)
@@ -80,8 +93,11 @@
         if events and (begin is None or min(events)[0] <= begin[0]):
             event = min(events)
             events.remove(event)
-            time, _, colour, half, oy, oz, via = event
-            follow(time, colour, half, oy, oz, via)
+            time, number, colour, half, oy, oz, via, brings = event
+            before = count
+            follow(time, colour, half, oy, oz, via, brings)
+            if count > before or brings == "own" and COLOURS[colour][1]:
+                passed.add(number)
             continue
         time, link = begin
         item = min(
@@ -89,20 +105,22 @@
             key=lambda it: (it[1], it[0], it[2]),
         )
         waiting[link].remove(item)
-        known, _, _, colour, half, oy, oz = item
-        _, paired, halves = COLOURS[colour]
+        known, _, _, colour, half, oy, oz, sides = item
+        halves = COLOURS[colour][2]
         first, end = halves[half[0]][0], halves[half[-1]][1]
-        both = paired and link != "x"
-        free[link] = time + (end - first) * (2 if both else 1) * BLOCK_TILE / BYTES_PER_US
+        blocks = 2 if sides == "both" else 1
+        free[link] = time + (end - first) * blocks * BLOCK_TILE / BYTES_PER_US
         earlier = [b for b, s in zip(begun, sends) if s[0] == link]
         dy, dz = STEP[link]
-        sends.append((link, both, first, end, oy, oz))
+        sends.append((link, sides, first, end, oy, oz))
         begun.append(max([known] + earlier[-1:]))
         landed.append(free[link] + LATENCY)
-        events.append((landed[-1], count, colour, half, oy - dy, oz - dz, link))
-        count += 1
+        events.append((landed[-1], len(sends) - 1, colour, half, oy - dy, oz - dz, link, sides))
     steps = [(time, 1, index, "send") for index, time in enumerate(begun)]
-    steps += [(time, 0, index, "wait") for index, time in enumerate(landed)]
+    steps += [
+        (time + (0.0 if index in passed else SLACK), 0, index, "wait")
+        for index, time in enumerate(landed)
+    ]
     return sends, [(kind, index) for _, _, index, kind in sorted(steps)]
 
 
@@ -110,9 +128,11 @@
 
 
 def brought(index):
-    link, both, first, end, oy, oz = SENDS[index]
+    link, sides, first, end, oy, oz = SENDS[index]
     dy, dz = STEP[link]
-    sides = ("own", "other") if both else (("other",) if link == "x" else ("own",))
+    if link == "x":
+        sides = "other"
+    sides = ("own", "other") if sides == "both" else (sides,)
     return {
         (tile, (oy - dy) % Y_RING, (oz - dz) % Z_RING, side)
         for tile in range(first, end)
@@ -278,20 +298,32 @@
     }
 
 
-PIECES = [((6, 5), 25, 12, 12), ((4, 3), 9, 8, 8), ((2, 1, 0), 0, 5, 4)]
+PIECES = [
+    ((6,), 36, 7, 6),
+    ((5,), 25, 6, 5),
+    ((4,), 16, 5, 4),
+    ((3,), 9, 4, 3),
+    ((0, 1, 2), 0, 5, 4),
+]
+PART_ROWS = 16 * sum(piece[2] for piece in PIECES)
 
 
 def layer_kernel(
+    nodes_hbm,
+    vector_hbm,
+    part_hbm,
+    slot_hbm,
+    target_hbm,
+    live_ref,
+    zero_hbm,
+    one_hbm,
+    two_hbm,
+    out_ref,
     nodes_ref,
     vector_ref,
     part_ref,
     slot_ref,
     target_ref,
-    live_ref,
-    zero_hbm,
-    one_hbm,
-    two_hbm,
-    out_ref,
     table_ref,
     vectors_ref,
     zero_ref,
@@ -302,7 +334,7 @@
     states_ref,
     rows_ref,
     left_ref,
-    sum_ref,
+    mixed_ref,
     parts_ref,
     landing_ref,
     send,
@@ -314,6 +346,20 @@
     edge = lax.axis_index("edge")
     chan = lax.axis_index("chan")
     edges = part_ref.shape[1]
+    reads = [
+        pltpu.make_async_copy(src, dst, local.at[3 + index])
+        for index, (src, dst) in enumerate(
+            (
+                (nodes_hbm, nodes_ref),
+                (vector_hbm, vector_ref),
+                (part_hbm, part_ref),
+                (slot_hbm, slot_ref),
+                (target_hbm, target_ref),
+            )
+        )
+    ]
+    for read in reads:
+        read.start()
     x = edge % 2
     z = (edge // 2) % Z_RING
     y = edge // (2 * Z_RING)
@@ -344,6 +390,8 @@
             ((one_hbm, one_ref), (two_hbm, two_ref), (zero_hbm, zero_ref))
         )
     ]
+    for read in reads:
+        read.wait()
     for tile in range(TILES):
         low = nodes_ref[tile]
         high = nodes_ref[tile + TILES] if tile + TILES < COEFS else jnp.zeros_like(low)
@@ -352,11 +400,12 @@
     pl.semaphore_wait(barrier, 8)
 
     copies = []
-    for index, (link, both, first, end, oy, oz) in enumerate(SENDS):
+    span = {"both": pl.ds(0, 2), "own": pl.ds(x, 1), "other": pl.ds(1 - x, 1)}
+    for index, (link, sides, first, end, oy, oz) in enumerate(SENDS):
         view = table_ref.at[
             wrap(y, oy, Y_RING),
             wrap(z, oz, Z_RING),
-            pl.ds(0, 2) if both else pl.ds(x, 1),
+            span[sides],
             pl.ds(first, end - first),
         ]
         copies.append(
@@ -494,45 +543,50 @@
         blocks = [left_ref[first // LANES + i] for i in range(-(-depth // LANES))]
         return jnp.concatenate(blocks, axis=1)[:, :depth]
 
-    def mix(order, degree, start, depth, right):
+    def mix(turn_of, order, start, depth, right):
         mixed = jnp.dot(left(start, depth), right, preferred_element_type=jnp.float32)
-        mixed = mixed.astype(jnp.bfloat16)
-        back = jnp.concatenate(
-            [
-                (rot_ref[degree * degree + k, order : order + 1, :] * chosen).astype(jnp.bfloat16)
-                for k in range(2 * degree + 1)
-            ],
-            axis=0,
-        )
-        rows = pl.ds(16 * degree * degree, 16 * (2 * degree + 1))
-        value = jnp.dot(back, mixed, preferred_element_type=jnp.float32)
-        sum_ref[rows, :] = value if order == 0 else sum_ref[rows, :] + value
+        mixed_ref[turn_of, order] = mixed.astype(jnp.bfloat16)
+
+    def degree_sum(degree, turn_of):
+        mix(turn_of, 0, STARTS["z"], 448, zero_ref[:, degree].reshape(448, 256))
+        if degree >= 1:
+            right = one_ref[:, :, degree - 1].reshape(768, 256)
+            mix(turn_of, 1, STARTS["p1"], 768, right)
+            mix(turn_of, 2, STARTS["n1"], 768, right)
+        if degree >= 2:
+            right = two_ref[:, :, degree - 2].reshape(640, 256)
+            mix(turn_of, 3, STARTS["p2"], 640, right)
+            mix(turn_of, 4, STARTS["n2"], 640, right)
+        orders = 2 * min(degree, MMAX) + 1
+        back = [
+            jnp.concatenate(
+                [
+                    (rot_ref[degree * degree + k, order : order + 1, :] * chosen).astype(
+                        jnp.bfloat16
+                    )
+                    for k in range(2 * degree + 1)
+                ],
+                axis=0,
+            )
+            for order in range(orders)
+        ]
+        back = jnp.concatenate(back, axis=1) if orders > 1 else back[0]
+        mixed = mixed_ref[turn_of, 0:orders].reshape(orders * edges, 256)
+        return jnp.dot(back, mixed, preferred_element_type=jnp.float32)
 
     for load in loads:
         load.wait()
     outgoing = []
     base = 0
     for number, (degrees, first, lows, highs) in enumerate(PIECES):
-        for degree in degrees:
-            mix(0, degree, STARTS["z"], 448, zero_ref[:, degree].reshape(448, 256))
-            if degree >= 1:
-                right = one_ref[:, :, degree - 1].reshape(768, 256)
-                mix(1, degree, STARTS["p1"], 768, right)
-                mix(2, degree, STARTS["n1"], 768, right)
-            if degree >= 2:
-                right = two_ref[:, :, degree - 2].reshape(640, 256)
-                mix(3, degree, STARTS["p2"], 640, right)
-                mix(4, degree, STARTS["n2"], 640, right)
+        sums = [degree_sum(degree, degree % 2) for degree in degrees]
+        sums = jnp.concatenate(sums, axis=0) if len(sums) > 1 else sums[0]
+        if highs < lows:
+            sums = jnp.concatenate([sums, jnp.zeros((16, 256), jnp.float32)], axis=0)
         for part in range(4):
-            lanes = pl.ds(64 * part, 64)
-            low = sum_ref[pl.ds(16 * first, 16 * lows), lanes]
-            high = sum_ref[pl.ds(16 * (first + lows), 16 * highs), lanes]
-            if highs < lows:
-                high = jnp.concatenate(
-                    [high, jnp.zeros((16 * (lows - highs), 64), jnp.float32)], axis=0
-                )
+            lanes = slice(64 * part, 64 * part + 64)
             parts_ref[part, pl.ds(16 * base, 16 * lows)] = jnp.concatenate(
-                [low, high], axis=1
+                [sums[: 16 * lows, lanes], sums[16 * lows :, lanes]], axis=1
             ).astype(jnp.bfloat16)
         piece = []
         for far in (2, 1, 3):
@@ -589,9 +643,14 @@
         layer_kernel,
         name="layer",
         out_shape=jax.ShapeDtypeStruct((COEFS, 16, 64), jnp.bfloat16),
-        in_specs=[vmem] * 5 + [pl.BlockSpec(memory_space=pltpu.SMEM), hbm, hbm, hbm],
+        in_specs=[hbm] * 5 + [pl.BlockSpec(memory_space=pltpu.SMEM), hbm, hbm, hbm],
         out_specs=vmem,
         scratch_shapes=[
+            pltpu.VMEM((COEFS, 16, 64), jnp.bfloat16),
+            pltpu.VMEM((3, LANES), jnp.float32),
+            pltpu.VMEM((1, edges), jnp.int32),
+            pltpu.VMEM((1, edges), jnp.int32),
+            pltpu.VMEM((1, edges), jnp.int32),
             pltpu.VMEM((Y_RING, Z_RING, 2, TILES, 16, LANES), jnp.bfloat16),
             pltpu.VMEM((4, 3, LANES), jnp.float32),
             pltpu.VMEM(zero.shape, jnp.bfloat16),
@@ -602,14 +661,14 @@
             pltpu.VMEM((TILES * LANES, edges), jnp.bfloat16),
             pltpu.VMEM((LEFT_BLOCKS * LANES, edges), jnp.bfloat16),
             pltpu.VMEM((LEFT_BLOCKS, edges, LANES), jnp.bfloat16),
-            pltpu.VMEM((16 * COEFS, 256), jnp.float32),
-            pltpu.VMEM((4, 400, LANES), jnp.bfloat16),
-            pltpu.VMEM((3, 400, LANES), jnp.bfloat16),
+            pltpu.VMEM((2, 5, edges, 256), jnp.bfloat16),
+            pltpu.VMEM((4, PART_ROWS, LANES), jnp.bfloat16),
+            pltpu.VMEM((3, PART_ROWS, LANES), jnp.bfloat16),
             pltpu.SemaphoreType.DMA((len(SENDS),)),
             pltpu.SemaphoreType.DMA((len(SENDS),)),
-            pltpu.SemaphoreType.DMA((3,)),
+            pltpu.SemaphoreType.DMA((8,)),
             pltpu.SemaphoreType.DMA((6,)),
-            pltpu.SemaphoreType.DMA((2, 3, 3)),
+            pltpu.SemaphoreType.DMA((2, len(PIECES), 3)),
         ],
         compiler_params=pltpu.CompilerParams(
             collective_id=0, has_side_effects=True, vmem_limit_bytes=60 << 20

time: 76.8 us -> 70 us (0.911)
  Pallas kernels: 74.4 us -> 67.6 us
    pallas_call x1, Pallas kernels: 74.4 us -> 67.6 us  [shards(): pl.pallas_call(layer_kernel, name='layer', out_shape=jax.ShapeDtypeStruct...]
where the time goes in v4:
time: 70 us; the launch traced here: 69.9 us
  Pallas kernels  67.6 us (97%)
  local copies, waits for them, and re-layouts  1.62 us (2%)
    pallas_call x1, Pallas kernels, shards(): pl.pallas_call(layer_kernel, name='layer', out_shape=jax.ShapeDtypeStruct...  67.6 us
    unnamed x1, local copies, waits for them, and re-layouts  1.62 us

profile of v4, /device:TPU:1, one launch (start us, length us, event | category | flops | bytes accessed | tf_op | source)
XLA Modules:
  0.0 69.9 jit_solution(14190059664256922454)
XLA Ops:
  0.7 67.6 %layer.1 = bf16[49,16,64]{2,1,0:T(8,128)(2,1)} custom-call(bf16[49,16,64]{2,1,0:T(8,128)(2,1)} %bitcast.12, f32[3,128]{1,0:T(4,128)} %vector_hbm.1, s32[1,512]{1,0:T(1,128)} %bitcast.13, s32[1,512]{1,0:T(1,128)} %bitcast.14, s32[1,512]{1,0:T(1,128)} %bitcast.15, s32[1]{0:T(128)S(6)} %copy.11.live_ref, bf16[7,7,64,256]{3,2,1,0:T(8,128)(2,1)} %bitcast.10, ...), custom_call_target="tpu_custom_call" | custom-call | tf_op jit(solution)/shard_map/layer/pallas_call | solution.py:642
  68.3 1.6 %copy.12 = bf16[16,49,64]{2,0,1:T(8,128)(2,1)} copy(bf16[16,49,64]{2,0,1:T(8,128)(2,1)} %bitcast.11) | data formatting | bytes 200704

commit v5 on v4

--- a/solution.py
+++ b/solution.py
@@ -25,7 +25,7 @@
     "sz": ("z", False, ((19, 22), (22, 25))),
 }
 Y_TILES = 10
-LATENCY, BYTES_PER_US, BLOCK_TILE, SLACK = 2.8, 46e3, 4096, 3.0
+LATENCY, BYTES_PER_US, BLOCK_TILE, SLACK = 2.8, 46e3, 4096, 1.0
 
 
 def schedule():
@@ -603,6 +603,8 @@
             piece.append(copy)
         outgoing.append((base, piece))
         base += lows
+    for copy in copies + spread:
+        copy.wait_send()
     for (base, piece), (degrees, first, lows, highs) in zip(outgoing, PIECES):
         for copy in piece:
             copy.wait_recv()
@@ -615,8 +617,6 @@
             out_ref[first + step] = total[16 * step : 16 * step + 16, :64]
         for step in range(highs):
             out_ref[first + lows + step] = total[16 * step : 16 * step + 16, 64:]
-    for copy in copies + spread:
-        copy.wait_send()
     for _, piece in outgoing:
         for copy in piece:
             copy.wait_send()

time: 70 us -> 69.4 us (level)
  no operation moved by 1% of the time
where the time goes in v5:
time: 69.4 us; the launch traced here: 69.3 us
  Pallas kernels  67 us (97%)
  local copies, waits for them, and re-layouts  1.62 us (2%)
    pallas_call x1, Pallas kernels, shards(): pl.pallas_call(layer_kernel, name='layer', out_shape=jax.ShapeDtypeStruct...  67 us
    unnamed x1, local copies, waits for them, and re-layouts  1.62 us

profile of v5, /device:TPU:1, one launch (start us, length us, event | category | flops | bytes accessed | tf_op | source)
XLA Modules:
  0.0 69.3 jit_solution(15460402110713212013)
XLA Ops:
  0.7 67.0 %layer.1 = bf16[49,16,64]{2,1,0:T(8,128)(2,1)} custom-call(bf16[49,16,64]{2,1,0:T(8,128)(2,1)} %bitcast.12, f32[3,128]{1,0:T(4,128)} %vector_hbm.1, s32[1,512]{1,0:T(1,128)} %bitcast.13, s32[1,512]{1,0:T(1,128)} %bitcast.14, s32[1,512]{1,0:T(1,128)} %bitcast.15, s32[1]{0:T(128)S(6)} %copy.11.live_ref, bf16[7,7,64,256]{3,2,1,0:T(8,128)(2,1)} %bitcast.10, ...), custom_call_target="tpu_custom_call" | custom-call | tf_op jit(solution)/shard_map/layer/pallas_call | solution.py:642
  67.6 1.6 %copy.12 = bf16[16,49,64]{2,0,1:T(8,128)(2,1)} copy(bf16[16,49,64]{2,0,1:T(8,128)(2,1)} %bitcast.11) | data formatting | bytes 200704
